TPU v7x, 16 devices: a 4x2x1 block of a 4x4x8 slice. The times are simulated.
16 devices in a mesh: rep: 2 (over y, z), dp: 8 (over x, core).
Axes of the slice: x: 4, y: 2, z: 1, core: 2. Of those that a mesh axis runs over, the one named last changes fastest.
The devices are a block of a 4x4x8 slice.
Arguments:
- x: bfloat16 [16, 2048, 640], P(('rep', 'dp')), parts along dimension 0
- dy: bfloat16 [16, 2048, 640], P(('rep', 'dp')), parts along dimension 0
- w_gate: bfloat16 [2, 640, 3200], replicated
- w_up: bfloat16 [2, 640, 3200], replicated
- w_down: bfloat16 [2, 3200, 640], replicated
- m_w_gate: float32 [2, 640, 3200], P(None, 'dp')
- m_w_up: float32 [2, 640, 3200], P(None, 'dp')
- m_w_down: float32 [2, 3200, 640], P(None, 'dp')
- v_w_gate: float32 [2, 640, 3200], P(None, 'dp')
- v_w_up: float32 [2, 640, 3200], P(None, 'dp')
- v_w_down: float32 [2, 3200, 640], P(None, 'dp')
Outputs:
- output 1: bfloat16 [4, 640, 3200], P('rep'), parts along dimension 0
- output 2: bfloat16 [4, 640, 3200], P('rep'), parts along dimension 0
- output 3: bfloat16 [4, 3200, 640], P('rep'), parts along dimension 0
- output 4: float32 [4, 640, 3200], P('rep', 'dp'), parts along dimension 0
- output 5: float32 [4, 640, 3200], P('rep', 'dp'), parts along dimension 0
- output 6: float32 [4, 3200, 640], P('rep', 'dp'), parts along dimension 0
- output 7: float32 [4, 640, 3200], P('rep', 'dp'), parts along dimension 0
- output 8: float32 [4, 640, 3200], P('rep', 'dp'), parts along dimension 0
- output 9: float32 [4, 3200, 640], P('rep', 'dp'), parts along dimension 0
There are 2 independent parts. A program takes and returns all parts, laid end to end along the dimension named above; an argument that names none is the same for every part.
All inputs are finite; a program needn't handle non-finite values.
Results may differ from a plain program's by a relative error of at most 0.022.
Values are sent between devices in bfloat16 or wider.
A program may use at most 768 MiB of HBM per device.

v0:
```python
import jax
import jax.numpy as jnp
from jax import lax

NAMES = ("w_gate", "w_up", "w_down")


def matmul(a, w):
    return jnp.dot(a, w, preferred_element_type=jnp.float32).astype(jnp.bfloat16)


def normed(h):
    wide = h.astype(jnp.float32)
    scale = lax.rsqrt(jnp.mean(wide**2, -1, keepdims=True) + 1e-6)
    return (wide * scale).astype(jnp.bfloat16)


def layer(h, w):
    a = normed(h)
    gate = jnp.dot(a, w["w_gate"], preferred_element_type=jnp.float32)
    up = jnp.dot(a, w["w_up"], preferred_element_type=jnp.float32)
    return h + matmul((jax.nn.silu(gate) * up).astype(jnp.bfloat16), w["w_down"])


def adamw(w, m, v, g):
    m = 0.9 * m + 0.1 * g
    v = 0.95 * v + 0.05 * g * g
    step = m * lax.rsqrt(v + 1e-8) + 0.1 * w
    return (w - 0.02 * step).astype(jnp.bfloat16), m, v


def stack(weights, h):
    for number in range(weights["w_gate"].shape[0]):
        h = layer(h, {name: w[number] for name, w in weights.items()})
    return h


def solution(mesh):
    groups = mesh.shape["rep"]

    def step(x, dy, *arrays):
        weights, m, v = (arrays[i : i + 3] for i in (0, 3, 6))
        x, dy = (t.reshape(groups, -1, *t.shape[1:]) for t in (x, dy))

        def of_a_group(x, dy):
            _, back = jax.vjp(lambda w: stack(w, x), dict(zip(NAMES, weights, strict=True)))
            by_weights = back(dy)[0]
            gradients = [by_weights[name].astype(jnp.float32) for name in NAMES]
            new = [adamw(w.astype(jnp.float32), m, v, g) for w, m, v, g in zip(weights, m, v, gradients, strict=True)]
            return tuple(one[which] for which in range(3) for one in new)

        return tuple(t.reshape(-1, *t.shape[2:]) for t in jax.vmap(of_a_group)(x, dy))

    return step
```

profile of v0, /device:TPU:113, one launch (start us, length us, event | category | flops | bytes accessed | tf_op | source)
XLA Modules:
  0.0 683.0 jit_solution(10110038802689013591)
XLA Ops:
  7.3 2.5 fusion.47
  9.7 4.4 copy
  14.2 16.7 %fusion.67 = f32[2048,3200]{1,0:T(8,128)} fusion(bf16[2,640,3200]{2,1,0:T(8,128)(2,1)} %param, bf16[1,2048,640]{2,1,0:T(8,128)(2,1)S(1)} %copy-done, f32[2048]{0:T(1024)S(1)} %add_rsqrt_fusion), kind=kOutput, calls=%fused_computation.79 | convolution fusion | flops 8392540160 | bytes 32940032 | tf_op jit(solution)/vmap(jvp())/dot_general | solution.py:20
  30.9 16.6 %fusion.65 = f32[2048,3200]{1,0:T(8,128)} fusion(bf16[2,640,3200]{2,1,0:T(8,128)(2,1)} %param.3, bf16[1,2048,640]{2,1,0:T(8,128)(2,1)S(1)} %copy-done, f32[2048]{0:T(1024)S(1)} %add_rsqrt_fusion), kind=kOutput, calls=%fused_computation.77 | convolution fusion | flops 8392540160 | bytes 32940032 | tf_op jit(solution)/vmap(jvp())/dot_general | solution.py:21
  47.5 23.1 %fusion.26 = bf16[2048,3200]{1,0:T(8,128)(2,1)} fusion(f32[2048,3200]{1,0:T(8,128)} %fusion.65, f32[2048,3200]{1,0:T(8,128)} %fusion.67), kind=kLoop, calls=%fused_computation.37 | loop fusion | flops 39321600 | bytes 65536000
  70.6 13.6 %fusion.51 = (f32[2048]{0:T(1024)S(1)}, bf16[1,1,2048,640]{2,3,1,0:T(8,128)(2,1)S(1)}) fusion(bf16[2048,3200]{1,0:T(8,128)(2,1)} %fusion.26, bf16[2,3200,640]{2,1,0:T(8,128)(2,1)} %param.4, bf16[1,2048,640]{1,2,0:T(8,128)(2,1)S(1)} %copy-done.7), kind=kOutput, calls=%fused_computation.62 | convolution fusion | flops 8395159552 | bytes 22454272 | tf_op jit(solution)/vmap(jvp())/dot_general | solution.py:9
  84.3 17.2 %fusion.54 = f32[2048,3200]{1,0:T(8,128)} fusion(bf16[2,640,3200]{2,1,0:T(8,128)(2,1)} %param, bf16[1,1,2048,640]{2,3,1,0:T(8,128)(2,1)S(1)} %get-tuple-element.10, f32[2048]{0:T(1024)S(1)} %bitcast.374), kind=kOutput, calls=%fused_computation.66 | convolution fusion | flops 8392540160 | bytes 32940032 | tf_op jit(solution)/vmap(jvp())/dot_general | solution.py:20
  101.5 16.5 %fusion.58 = f32[2048,3200]{1,0:T(8,128)} fusion(bf16[2,640,3200]{2,1,0:T(8,128)(2,1)} %param.3, bf16[1,1,2048,640]{2,3,1,0:T(8,128)(2,1)S(1)} %get-tuple-element.10, f32[2048]{0:T(1024)S(1)} %bitcast.375), kind=kOutput, calls=%fused_computation.70 | convolution fusion | flops 8392540160 | bytes 32940032 | tf_op jit(solution)/vmap(jvp())/dot_general | solution.py:21
  118.0 15.5 %convolution_convert_fusion.1 = bf16[2048,3200]{1,0:T(8,128)(2,1)} fusion(bf16[2,3200,640]{2,1,0:T(8,128)(2,1)} %param.4, bf16[1,2048,640]{2,1,0:T(8,128)(2,1)S(1)} %copy-done.5), kind=kOutput, calls=%fused_computation.36 | convolution fusion | flops 8395161600 | bytes 19824640 | tf_op jit(solution)/vmap(transpose(jvp()))/dot_general | solution.py:9
  133.5 3.0 copy.1
  136.5 26.9 %fusion.6 = bf16[2048,3200]{1,0:T(8,128)(2,1)} fusion(f32[2048,3200]{1,0:T(8,128)} %fusion.54, f32[2048,3200]{1,0:T(8,128)} %fusion.58, bf16[2048,3200]{1,0:T(8,128)(2,1)} %convolution_convert_fusion.1), kind=kLoop, calls=%fused_computation.11 | loop fusion | flops 78643200 | bytes 78643200
  163.4 14.9 %fusion.81 = bf16[2048,640]{0,1:T(8,128)(2,1)} fusion(bf16[2048,3200]{1,0:T(8,128)(2,1)} %fusion.6, bf16[2,640,3200]{2,1,0:T(8,128)(2,1)} %param), kind=kOutput, calls=%fused_computation.91 | convolution fusion | flops 8388608000 | bytes 19824640 | tf_op jit(solution)/vmap(transpose(jvp()))/dot_general | solution.py:20
  178.3 21.4 %fusion.53 = (f32[2048]{0:T(1024)S(1)}, bf16[1,1,2048,640]{2,3,1,0:T(8,128)(2,1)}) fusion(bf16[1,1,2048,640]{2,3,1,0:T(8,128)(2,1)} %copy-done.1, bf16[2048,640]{0,1:T(8,128)(2,1)} %fusion.81, bf16[2,640,3200]{2,1,0:T(8,128)(2,1)} %param.3, bf16[2048,3200]{1,0:T(8,128)(2,1)} %convolution_convert_fusion.1, f32[2048,3200]{1,0:T(8,128)} %fusion.54), kind=kOutput, calls=%fused_computation.64 | convolution fusion | flops 8435791872 | bytes 51290112 | tf_op jit(solution)/vmap(transpose(jvp()))/dot_general | solution.py:21
  199.7 4.3 fusion.108
  204.1 1.5 copy-done.3
  205.6 12.8 %convolution_bitcast_fusion = f32[1,3200,640]{2,1,0:T(8,128)} fusion(bf16[2048,3200]{1,0:T(8,128)(2,1)S(1)} %bitcast.365, bf16[2048,640]{0,1:T(8,128)(2,1)S(1)} %fusion.108), kind=kOutput, calls=%fused_computation.51 | convolution fusion | flops 8388608000 | bytes 23920640 | tf_op jit(solution)/vmap(transpose(jvp()))/dot_general | solution.py:9
  218.4 0.1 reduce-scatter.27.cloned.1.call-start
  218.5 1.6 copy-done.6
  220.1 23.3 %fusion.41 = f32[1,3200,640]{2,1,0:T(8,128)} fusion(f32[2048,3200]{1,0:T(8,128)} %fusion.58, f32[2048,3200]{1,0:T(8,128)} %fusion.54, bf16[1,2048,640]{2,1,0:T(8,128)(2,1)S(1)} %copy-done.6), kind=kOutput, calls=%fused_computation.53 | convolution fusion | flops 8427929600 | bytes 63242240 | tf_op jit(solution)/vmap(transpose(jvp()))/dot_general | solution.py:9
  243.5 1.6 copy-done.4
  245.1 15.3 %convolution_convert_fusion = bf16[2048,3200]{1,0:T(8,128)(2,1)} fusion(bf16[2048,640]{0,1:T(8,128)(2,1)S(1)} %copy-done.4, bf16[2,3200,640]{2,1,0:T(8,128)(2,1)} %param.4), kind=kOutput, calls=%fused_computation.35 | convolution fusion | flops 8395161600 | bytes 19824640 | tf_op jit(solution)/vmap(transpose(jvp()))/dot_general | solution.py:9
  260.3 20.5 %fusion.38 = f32[1,640,3200]{2,1,0:T(8,128)} fusion(bf16[2048,3200]{1,0:T(8,128)(2,1)} %convolution_convert_fusion, f32[2048,3200]{1,0:T(8,128)} %fusion.67, bf16[1,2048,640]{1,2,0:T(8,128)(2,1)} %copy, f32[2048]{0:T(1024)S(1)} %copy-done.13), kind=kOutput, calls=%fused_computation.50 | convolution fusion | flops 8431861760 | bytes 50143232 | tf_op jit(solution)/vmap(transpose(jvp()))/dot_general | solution.py:21
  281.0 1.6 copy-done.2
  282.6 19.7 %fusion.35 = f32[1,640,3200]{2,1,0:T(8,128)} fusion(bf16[2048,3200]{1,0:T(8,128)(2,1)} %convolution_convert_fusion.1, f32[2048,3200]{1,0:T(8,128)} %fusion.54, bf16[1,1,2048,640]{2,3,1,0:T(8,128)(2,1)S(1)} %copy-done.2, f32[2048]{0:T(1024)S(1)} %bitcast.377), kind=kOutput, calls=%fused_computation.49 | convolution fusion | flops 8431861760 | bytes 50143232 | tf_op jit(solution)/vmap(transpose(jvp()))/dot_general | solution.py:21
  302.4 14.7 %convolution_bitcast_fusion.1 = f32[1,640,3200]{2,1,0:T(8,128)} fusion(bf16[2048,3200]{1,0:T(8,128)(2,1)} %fusion.6, bf16[1,1,2048,640]{2,3,1,0:T(8,128)(2,1)S(1)} %copy-done.2, f32[2048]{0:T(1024)S(1)} %bitcast.378), kind=kOutput, calls=%fused_computation.52 | convolution fusion | flops 8392540160 | bytes 23928832 | tf_op jit(solution)/vmap(transpose(jvp()))/dot_general | solution.py:20
  317.3 1.6 copy-done.8
  318.9 27.1 %fusion.44 = f32[1,640,3200]{2,1,0:T(8,128)} fusion(f32[2048,3200]{1,0:T(8,128)} %fusion.67, f32[2048,3200]{1,0:T(8,128)} %fusion.65, bf16[2048,3200]{1,0:T(8,128)(2,1)} %convolution_convert_fusion, bf16[1,2048,640]{1,2,0:T(8,128)(2,1)S(1)} %copy-done.8, f32[2048]{0:T(1024)S(1)} %copy-done.13), kind=kOutput, calls=%fused_computation.54 | convolution fusion | flops 8464629760 | bytes 76357632 | tf_op jit(solution)/vmap(transpose(jvp()))/dot_general | solution.py:20
  346.2 0.5 copy-done.14
  346.7 0.6 dynamic-slice
  348.0 1.3 convert_bitcast_fusion.3
  349.3 1.3 convert_bitcast_fusion.4
  350.5 5.3 fusion.144
  356.0 12.1 %reduce-scatter.25.cloned.1.call-done = f32[1,80,3200]{2,1,0:T(8,128)} async-done(((f32[1,640,3200]{2,1,0:T(8,128)}), f32[1,80,3200]{2,1,0:T(8,128)}) %reduce-scatter.25.cloned.1.call-update) | async-done | bytes 1024016
  368.1 1.3 convert_bitcast_fusion.5
  369.4 48.1 %reduce-scatter.23.cloned.1.call-done = f32[1,80,3200]{2,1,0:T(8,128)} async-done(((f32[1,640,3200]{2,1,0:T(8,128)}), f32[1,80,3200]{2,1,0:T(8,128)}) %reduce-scatter.23.cloned.1.call-update) | async-done | bytes 1024016
  417.4 1.3 convert_bitcast_fusion.6
  418.7 5.2 fusion.145
  424.1 43.2 %reduce-scatter.19.cloned.1.call-done = f32[1,80,3200]{2,1,0:T(8,128)} async-done(((f32[1,640,3200]{2,1,0:T(8,128)}), f32[1,80,3200]{2,1,0:T(8,128)}) %reduce-scatter.19.cloned.1.call-update) | async-done | bytes 1024016
  467.3 1.3 convert_bitcast_fusion.8
  468.6 48.6 %reduce-scatter.21.cloned.1.call-done = f32[1,80,3200]{2,1,0:T(8,128)} async-done(((f32[1,640,3200]{2,1,0:T(8,128)}), f32[1,80,3200]{2,1,0:T(8,128)}) %reduce-scatter.21.cloned.1.call-update) | async-done | bytes 1024016
  517.3 1.3 convert_bitcast_fusion.7
  518.5 5.3 fusion.146
  523.9 40.1 %all-gather.14.cloned.1.call-done = bf16[1,2,3200,640]{3,2,1,0:T(8,128)(2,1)} async-done(((bf16[1,2,400,640]{3,2,1,0:T(8,128)(2,1)}), bf16[1,2,3200,640]{3,2,1,0:T(8,128)(2,1)}) %all-gather.14.cloned.1.call-update) | async-done | bytes 8192016 | tf_op jit(solution)/reshape | solution.py:52
  564.0 47.0 %all-gather.12.cloned.1.call-done = bf16[1,2,640,3200]{3,2,1,0:T(8,128)(2,1)} async-done(((bf16[1,2,80,3200]{3,2,1,0:T(8,128)(2,1)}), bf16[1,2,640,3200]{3,2,1,0:T(8,128)(2,1)}) %all-gather.12.cloned.1.call-update) | async-done | bytes 8192016 | tf_op jit(solution)/reshape | solution.py:52
  611.0 47.0 %all-gather.10.cloned.1.call-done = bf16[1,2,640,3200]{3,2,1,0:T(8,128)(2,1)} async-done(((bf16[1,2,80,3200]{3,2,1,0:T(8,128)(2,1)}), bf16[1,2,640,3200]{3,2,1,0:T(8,128)(2,1)}) %all-gather.10.cloned.1.call-update) | async-done | bytes 8192016 | tf_op jit(solution)/reshape | solution.py:52
  658.0 7.4 %copy.5 = bf16[2,640,3200]{2,1,0:T(8,128)(2,1)} copy(bf16[2,640,3200]{2,1,0:T(8,128)(2,1)} %bitcast.370) | data formatting | bytes 16384000
  665.3 7.4 %copy.6 = bf16[2,640,3200]{2,1,0:T(8,128)(2,1)} copy(bf16[2,640,3200]{2,1,0:T(8,128)(2,1)} %bitcast.369) | data formatting | bytes 16384000
  672.7 3.3 copy.7
  (61 shorter events, 1.2 us)
Async XLA Ops:
  7.2 6.9 %copy-start = (bf16[1,2048,640]{2,1,0:T(8,128)(2,1)S(1)}, bf16[1,2048,640]{2,1,0:T(8,128)(2,1)}, u32[]{:S(2)}) copy-start(bf16[1,2048,640]{2,1,0:T(8,128)(2,1)} %param.2) | copy-start | bytes 7864324
  7.2 340.7 %reduce-scatter.29.cloned.1.call-start = ((), (), s32[]{:S(2)}) async-start(), calls=%async_computation.14 | async-start | bytes 9216000
  14.1 16.8 %copy-start.12 = (f32[2048]{0:T(1024)}, f32[2048]{0:T(1024)S(1)}, u32[]{:S(2)}) copy-start(f32[2048]{0:T(1024)S(1)} %add_rsqrt_fusion) | copy-start | bytes 24580
  47.5 23.1 %copy-start.7 = (bf16[1,2048,640]{1,2,0:T(8,128)(2,1)S(1)}, bf16[1,2048,640]{1,2,0:T(8,128)(2,1)}, u32[]{:S(2)}) copy-start(bf16[1,2048,640]{1,2,0:T(8,128)(2,1)} %copy) | copy-start | bytes 7864324
  84.3 17.2 %copy-start.1 = (bf16[1,1,2048,640]{2,3,1,0:T(8,128)(2,1)}, bf16[1,1,2048,640]{2,3,1,0:T(8,128)(2,1)S(1)}, u32[]{:S(2)}) copy-start(bf16[1,1,2048,640]{2,3,1,0:T(8,128)(2,1)S(1)} %get-tuple-element.10) | copy-start | bytes 7864324
  101.5 16.5 %copy-start.5 = (bf16[1,2048,640]{2,1,0:T(8,128)(2,1)S(1)}, bf16[1,2048,640]{2,1,0:T(8,128)(2,1)}, u32[]{:S(2)}) copy-start(bf16[1,2048,640]{2,1,0:T(8,128)(2,1)} %param.5) | copy-start | bytes 7864324
  163.4 42.2 %slice-start = ((s8[13107200]{0:T(1024)(128)(4,1)}), s8[4194304]{0:T(1024)(128)(4,1)S(1)}, s32[]{:S(2)}) async-start(s8[13107200]{0:T(1024)(128)(4,1)} %bitcast.364), calls=%async_computation.15 | async-start | bytes 8388608
  178.3 27.3 %slice-start.1 = ((s8[13107200]{0:T(1024)(128)(4,1)}), s8[4194304]{0:T(1024)(128)(4,1)S(1)}, s32[]{:S(2)}) async-start(s8[13107200]{0:T(1024)(128)(4,1)} %bitcast.364), calls=%async_computation.16 | async-start | bytes 8388608
  178.3 27.3 %slice-start.2 = ((s8[13107200]{0:T(1024)(128)(4,1)}), s8[4194304]{0:T(1024)(128)(4,1)S(1)}, s32[]{:S(2)}) async-start(s8[13107200]{0:T(1024)(128)(4,1)} %bitcast.364), calls=%async_computation.17 | async-start | bytes 8388608
  178.3 27.3 %slice-start.3 = ((s8[13107200]{0:T(1024)(128)(4,1)}), s8[524288]{0:T(1024)(128)(4,1)S(1)}, s32[]{:S(2)}) async-start(s8[13107200]{0:T(1024)(128)(4,1)} %bitcast.364), calls=%async_computation.18 | async-start | bytes 1048576
  204.1 1.5 copy-start.3
  218.4 1.7 copy-start.6
  218.4 130.8 %reduce-scatter.27.cloned.1.call-start = ((), (), s32[]{:S(2)}) async-start(), calls=%async_computation.13 | async-start | bytes 9216000
  243.3 1.7 copy-start.4
  243.4 16.9 %copy-start.13 = (f32[2048]{0:T(1024)S(1)}, f32[2048]{0:T(1024)}, u32[]{:S(2)}) copy-start(f32[2048]{0:T(1024)} %copy-done.12) | copy-start | bytes 24580
  243.4 124.7 %reduce-scatter.25.cloned.1.call-start = ((), (), s32[]{:S(2)}) async-start(), calls=%async_computation.12 | async-start | bytes 9216000
  280.9 1.7 copy-start.2
  280.9 136.5 %reduce-scatter.23.cloned.1.call-start = ((), (), s32[]{:S(2)}) async-start(), calls=%async_computation.11 | async-start | bytes 9216000
  302.4 165.0 %reduce-scatter.19.cloned.1.call-start = ((), (), s32[]{:S(2)}) async-start(), calls=%async_computation.9 | async-start | bytes 9216000
  317.1 1.7 copy-start.8
  317.2 200.1 %reduce-scatter.21.cloned.1.call-start = ((), (), s32[]{:S(2)}) async-start(), calls=%async_computation.10 | async-start | bytes 9216000
  346.0 0.7 copy-start.14
  346.0 4.5 copy-start.9
  346.1 217.9 %all-gather.14.cloned.1.call-start = ((), (), s32[]{:S(2)}) async-start(), calls=%async_computation.8 | async-start | bytes 9216000 | tf_op jit(solution)/reshape | solution.py:52
  355.8 62.9 %copy-start.10 = (f32[2,80,3200]{2,1,0:T(8,128)S(1)}, f32[2,80,3200]{2,1,0:T(8,128)}, u32[]{:S(2)}) copy-start(f32[2,80,3200]{2,1,0:T(8,128)} %param.8) | copy-start | bytes 6144004
  355.9 255.1 %all-gather.12.cloned.1.call-start = ((), (), s32[]{:S(2)}) async-start(), calls=%async_computation.7 | async-start | bytes 9216000 | tf_op jit(solution)/reshape | solution.py:52
  424.0 94.6 %copy-start.11 = (f32[2,80,3200]{2,1,0:T(8,128)S(1)}, f32[2,80,3200]{2,1,0:T(8,128)}, u32[]{:S(2)}) copy-start(f32[2,80,3200]{2,1,0:T(8,128)} %param.6) | copy-start | bytes 6144004
  424.0 234.0 %all-gather.10.cloned.1.call-start = ((), (), s32[]{:S(2)}) async-start(), calls=%async_computation.6 | async-start | bytes 9216000 | tf_op jit(solution)/reshape | solution.py:52
  658.0 14.7 %slice-start.4 = ((s8[8192000]{0:T(1024)(128)(4,1)}), s8[4194304]{0:T(1024)(128)(4,1)S(1)}, s32[]{:S(2)}) async-start(s8[8192000]{0:T(1024)(128)(4,1)} %bitcast.366), calls=%async_computation.19 | async-start | bytes 8388608
  665.3 7.4 %slice-start.5 = ((s8[8192000]{0:T(1024)(128)(4,1)}), s8[3997696]{0:T(1024)(128)(4,1)S(1)}, s32[]{:S(2)}) async-start(s8[8192000]{0:T(1024)(128)(4,1)} %bitcast.366), calls=%async_computation.20 | async-start | bytes 7995392
Sparse Core Ops, SparseCore 0:
  218.5 49.9 reduce-scatter.28
  270.8 47.1 reduce-scatter.26
  320.9 47.1 reduce-scatter.24
  370.2 47.1 reduce-scatter.22
  420.2 47.1 reduce-scatter.18
  470.1 47.1 reduce-scatter.20
  518.8 45.0 all-gather.13
  566.1 44.7 all-gather.11
  613.1 44.7 all-gather.9
where the time goes:
time: 692 us; the launch traced here: 683 us
  waiting for transfers between devices  287 us (41%)
  matrix products  266 us (38%)
  other arithmetic  80.2 us (12%)
  local copies, waits for them, and re-layouts  34.5 us (5%)
  between operations  15.2 us (2%)
    unnamed x15, waiting for transfers between devices  153 us
    reshape x3, waiting for transfers between devices, step(): t.reshape(-1, *t.shape[2:])  134 us
    dot_general x5, matrix products, layer(): up = jnp.dot(a, w['w_up'], preferred_element_type=jnp.float32)  94.7 us
    dot_general x5, matrix products, layer(): gate = jnp.dot(a, w['w_gate'], preferred_element_type=jnp.float32)  90.7 us
    dot_general x5, matrix products, matmul(): jnp.dot(a, w, preferred_element_type=jnp.float32).astype(jnp.bfloat16)  80.5 us
    unnamed x5, other arithmetic  54.3 us
    unnamed x47, local copies, waits for them, and re-layouts  33.9 us
    reshape x3, other arithmetic, step(): t.reshape(-1, *t.shape[2:])  15.8 us
  transfers between devices with their start and end apart: 9, of which 7 were waited for; matrix products, arithmetic and copies ran while one was open for 21% of the time, Pallas kernels for 0%

commit v1 on v0

v1 whole, which is shorter than its diff:
```python
import jax
import jax.numpy as jnp
from jax import lax
from jax.sharding import PartitionSpec as P

NAMES = ("w_gate", "w_up", "w_down")


def dot(a, b, dims):
    return lax.dot_general(a, b, (dims, ((), ())), preferred_element_type=jnp.float32)


def normed(h):
    wide = h.astype(jnp.float32)
    scale = lax.rsqrt(jnp.mean(wide**2, -1, keepdims=True) + 1e-6)
    return (wide * scale).astype(jnp.bfloat16)


def halves(h, wg, wu):
    a = normed(h)
    gate, up = dot(a, wg, ((1,), (0,))), dot(a, wu, ((1,), (0,)))
    return a, gate, up


def of_mid(dmid, gate, up):
    s = jax.nn.sigmoid(gate)
    silu = gate * s
    wide = dmid.astype(jnp.float32)
    dup = wide * silu
    dgate = wide * up * (s * (1 + gate * (1 - s)))
    return dgate.astype(jnp.bfloat16), dup.astype(jnp.bfloat16)


def adamw(w, m, v, g):
    m = 0.9 * m + 0.1 * g
    v = 0.95 * v + 0.05 * g * g
    step = m * lax.rsqrt(v + 1e-8) + 0.1 * w
    return (w - 0.02 * step).astype(jnp.bfloat16), m, v


def solution(mesh):
    def body(x, dy, *arrays):
        weights, ms, vs = (dict(zip(NAMES, arrays[i : i + 3])) for i in (0, 3, 6))
        x, dy = x[0], dy[0]
        layers = weights["w_gate"].shape[0]
        me = lax.axis_index("dp")

        kept, h = [], x
        for n in range(layers):
            wg, wu, wd = (weights[k][n] for k in NAMES)
            a, gate, up = halves(h, wg, wu)
            mid = (jax.nn.silu(gate) * up).astype(jnp.bfloat16)
            kept.append((h, a, gate, up, mid))
            if n < layers - 1:
                h = h + dot(mid, wd, ((1,), (0,))).astype(jnp.bfloat16)

        new = {}

        def finish(k, n, g):
            g = lax.psum_scatter(g.astype(jnp.bfloat16), "dp", scatter_dimension=0, tiled=True)
            rows = g.shape[0]
            w = lax.dynamic_slice_in_dim(weights[k][n], me * rows, rows, 0)
            w, m, v = adamw(w.astype(jnp.float32), ms[k][n], vs[k][n], g.astype(jnp.float32))
            new[k, n] = lax.all_gather(w, "dp", axis=0, tiled=True), m, v

        d = dy
        for n in reversed(range(layers)):
            wg, wu, wd = (weights[k][n] for k in NAMES)
            h, a, gate, up, mid = kept[n]
            finish("w_down", n, dot(mid, d, ((0,), (0,))))
            dmid = dot(d, wd, ((1,), (1,))).astype(jnp.bfloat16)
            dgate, dup = of_mid(dmid, gate, up)
            finish("w_gate", n, dot(a, dgate, ((0,), (0,))))
            finish("w_up", n, dot(a, dup, ((0,), (0,))))
            if n:
                da = dot(dgate, wg, ((1,), (1,))).astype(jnp.bfloat16) + dot(dup, wu, ((1,), (1,))).astype(jnp.bfloat16)
                _, back = jax.vjp(normed, h)
                d = d + back(da)[0]
        return tuple(jnp.stack([new[k, n][i] for n in range(layers)]) for i in range(3) for k in NAMES)

    rows = P(None, "dp", None)
    seqs = P(("rep", "dp"), None, None)
    return jax.shard_map(
        body,
        mesh=mesh,
        in_specs=(seqs, seqs, P(), P(), P()) + (rows,) * 6,
        out_specs=(P("rep", None, None),) * 3 + (P("rep", "dp", None),) * 6,
        check_vma=False,
    )
```

time: 692 us -> 592 us (0.86)
  waiting for transfers between devices: 287 us -> 210 us
  other arithmetic: 80.2 us -> 49.5 us
  matrix products: 266 us -> 284 us
  local copies, waits for them, and re-layouts: 34.5 us -> 26.1 us
    unnamed x15 -> x12, waiting for transfers between devices: 153 us -> 2.18 us
    all_gather x0 -> x6, waiting for transfers between devices: none -> 144 us  [finish(): new[k, n] = (lax.all_gather(w, 'dp', axis=0, tiled=True), m, v)]
    reshape x3 -> x0, waiting for transfers between devices: 134 us -> none  [step(): t.reshape(-1, *t.shape[2:])]
    reduce_scatter x0 -> x6, waiting for transfers between devices: none -> 63.2 us  [finish(): lax.psum_scatter(g.astype(jnp.bfloat16), 'dp', scatter_dimension=0, tiled...]
    unnamed x5 -> x0, other arithmetic: 54.3 us -> none
    another operation x0 -> x6, other arithmetic: none -> 30.9 us  [body(): jnp.stack([new[k, n][i] for n in range(layers)])]
    unnamed x47 -> x34, local copies, waits for them, and re-layouts: 33.9 us -> 8.72 us
    dot_general x15, matrix products: 266 us -> 284 us  [dot(): lax.dot_general(a, b, (dims, ((), ())), preferred_element_type=jnp.float32)]
  transfers between devices with their start and end apart: 9 -> 12, of which waited for: 7 -> 9; matrix products, arithmetic and copies ran while one was open for 21% -> 30% of each run, Pallas kernels for 0% -> 0%
where the time goes in v1:
time: 592 us; the launch traced here: 585 us
  matrix products  284 us (48%)
  waiting for transfers between devices  210 us (35%)
  other arithmetic  49.5 us (8%)
  local copies, waits for them, and re-layouts  26.1 us (4%)
  between operations  14.6 us (2%)
    dot_general x15, matrix products, dot(): lax.dot_general(a, b, (dims, ((), ())), preferred_element_type=jnp.float32)  284 us
    all_gather x6, waiting for transfers between devices, finish(): new[k, n] = (lax.all_gather(w, 'dp', axis=0, tiled=True), m, v)  144 us
    reduce_scatter x6, waiting for transfers between devices, finish(): lax.psum_scatter(g.astype(jnp.bfloat16), 'dp', scatter_dimension=0, tiled...  63.2 us
    another operation x6, other arithmetic, body(): jnp.stack([new[k, n][i] for n in range(layers)])  30.9 us
    convert_element_type x3, other arithmetic, adamw(): return ((w - 0.02 * step).astype(jnp.bfloat16), m, v)  16.2 us
  transfers between devices with their start and end apart: 12, of which 9 were waited for; matrix products, arithmetic and copies ran while one was open for 30% of the time, Pallas kernels for 0%

profile of v1, /device:TPU:113, one launch (start us, length us, event | category | flops | bytes accessed | tf_op | source)
XLA Modules:
  0.0 585.1 jit_solution(14185403286152431656)
XLA Ops:
  7.3 3.0 copy.20
  10.3 0.6 fusion.20
  10.8 18.6 %fusion.42 = f32[2048,3200]{1,0:T(8,128)} fusion(bf16[1,2048,640]{2,1,0:T(8,128)(2,1)} %param.11, f32[2048]{0:T(1024)S(1)} %add_rsqrt_fusion, bf16[2,640,3200]{2,1,0:T(8,128)(2,1)} %param.13), kind=kOutput, calls=%fused_computation.58 | convolution fusion | flops 8392540160 | bytes 32940032 | tf_op jit(solution)/shard_map/dot_general | solution.py:10
  29.5 28.0 %multiply_convert_fusion.1 = (bf16[2048,3200]{1,0:T(8,128)(2,1)}, f32[2048,3200]{1,0:T(8,128)}) fusion(f32[2048,3200]{1,0:T(8,128)} %fusion.42, bf16[2,640,3200]{2,1,0:T(8,128)(2,1)} %param.14, bf16[1,2048,640]{2,1,0:T(8,128)(2,1)} %param.11, f32[2048]{0:T(1024)S(1)} %add_rsqrt_fusion), kind=kOutput, calls=%fused_computation.13 | convolution fusion | flops 8431861760 | bytes 72261632 | tf_op jit(solution)/shard_map/dot_general | solution.py:10
  57.5 13.9 %fusion.24 = (f32[2048]{0:T(1024)S(1)}, bf16[2048,640]{0,1:T(8,128)(2,1)S(1)}) fusion(bf16[2048,3200]{1,0:T(8,128)(2,1)} %get-tuple-element.35, bf16[2,3200,640]{2,1,0:T(8,128)(2,1)} %param.15, bf16[1,2048,640]{1,2,0:T(8,128)(2,1)S(1)} %copy.20), kind=kOutput, calls=%fused_computation.41 | convolution fusion | flops 8395159552 | bytes 22454272 | tf_op jit(solution)/shard_map/dot_general | solution.py:10
  71.4 17.2 %fusion.35 = f32[2048,3200]{1,0:T(8,128)} fusion(bf16[2048,640]{0,1:T(8,128)(2,1)S(1)} %get-tuple-element.38, f32[2048]{0:T(1024)S(1)} %fusion.114, bf16[2,640,3200]{2,1,0:T(8,128)(2,1)} %param.14), kind=kOutput, calls=%fused_computation.51 | convolution fusion | flops 8392540160 | bytes 32940032 | tf_op jit(solution)/shard_map/dot_general | solution.py:10
  88.6 16.3 %fusion.31 = f32[2048,3200]{1,0:T(8,128)} fusion(bf16[2048,640]{0,1:T(8,128)(2,1)S(1)} %get-tuple-element.38, f32[2048]{0:T(1024)S(1)} %fusion.114, bf16[2,640,3200]{2,1,0:T(8,128)(2,1)} %param.13), kind=kOutput, calls=%fused_computation.47 | convolution fusion | flops 8392540160 | bytes 32940032 | tf_op jit(solution)/shard_map/dot_general | solution.py:10
  104.9 3.0 copy.21
  107.9 32.3 %fusion.2 = (bf16[2048,3200]{1,0:T(8,128)(2,1)}, bf16[2048,3200]{1,0:T(8,128)(2,1)}) fusion(f32[2048,3200]{1,0:T(8,128)} %fusion.31, f32[2048,3200]{1,0:T(8,128)} %fusion.35, bf16[2,3200,640]{2,1,0:T(8,128)(2,1)} %param.15, bf16[1,2048,640]{2,1,0:T(8,128)(2,1)} %param.12), kind=kOutput, calls=%fused_computation.6 | convolution fusion | flops 8486912000 | bytes 85360640 | tf_op jit(solution)/shard_map/dot_general | solution.py:10
  140.2 13.4 %fusion.48 = bf16[2048,640]{0,1:T(8,128)(2,1)S(1)} fusion(bf16[2048,3200]{1,0:T(8,128)(2,1)} %get-tuple-element.9, bf16[2,640,3200]{2,1,0:T(8,128)(2,1)} %param.14), kind=kOutput, calls=%fused_computation.62 | convolution fusion | flops 8389918720 | bytes 19824640 | tf_op jit(solution)/shard_map/dot_general | solution.py:10
  153.7 13.5 %fusion.26 = (f32[2048]{0:T(1024)S(1)}, bf16[2048,640]{0,1:T(8,128)(2,1)S(1)}) fusion(bf16[2048,640]{0,1:T(8,128)(2,1)S(1)} %copy-done.11, bf16[2048,640]{0,1:T(8,128)(2,1)S(1)} %fusion.48, bf16[2048,3200]{1,0:T(8,128)(2,1)} %get-tuple-element.10, bf16[2,640,3200]{2,1,0:T(8,128)(2,1)} %param.13), kind=kOutput, calls=%fused_computation.43 | convolution fusion | flops 8396470272 | bytes 25075712 | tf_op jit(solution)/shard_map/dot_general | solution.py:10
  167.2 1.8 fusion.61
  169.0 1.5 copy-done.13
  170.5 15.4 %convolution_convert_fusion.2 = bf16[3200,640]{1,0:T(8,128)(2,1)} fusion(bf16[2048,3200]{1,0:T(8,128)(2,1)} %get-tuple-element.35, bf16[2048,640]{0,1:T(8,128)(2,1)S(1)} %fusion.61), kind=kOutput, calls=%fused_computation.34 | convolution fusion | flops 8390656000 | bytes 19824640 | tf_op jit(solution)/shard_map/dot_general | solution.py:10
  186.1 23.0 %fusion.19 = bf16[3200,640]{1,0:T(8,128)(2,1)} fusion(f32[2048,3200]{1,0:T(8,128)} %fusion.35, f32[2048,3200]{1,0:T(8,128)} %fusion.31, bf16[1,2048,640]{2,1,0:T(8,128)(2,1)} %param.12), kind=kOutput, calls=%fused_computation.33 | convolution fusion | flops 8429977600 | bytes 59146240 | tf_op jit(solution)/shard_map/dot_general | solution.py:10
  209.2 14.1 %convolution_convert_fusion.3 = bf16[640,3200]{1,0:T(8,128)(2,1)} fusion(bf16[2048,3200]{1,0:T(8,128)(2,1)} %get-tuple-element.9, bf16[2048,640]{0,1:T(8,128)(2,1)S(1)} %copy-done.12, f32[2048]{0:T(1024)S(1)} %fusion.114), kind=kOutput, calls=%fused_computation.35 | convolution fusion | flops 8394588160 | bytes 19832832 | tf_op jit(solution)/shard_map/dot_general | solution.py:10
  223.5 16.6 %convolution_convert_fusion = bf16[2048,3200]{1,0:T(8,128)(2,1)} fusion(bf16[2048,640]{0,1:T(8,128)(2,1)} %copy-done.13, bf16[2,3200,640]{2,1,0:T(8,128)(2,1)} %param.15), kind=kOutput, calls=%fused_computation.16 | convolution fusion | flops 8395161600 | bytes 19824640 | tf_op jit(solution)/shard_map/dot_general | solution.py:10
  240.1 18.9 %fusion.16 = bf16[640,3200]{1,0:T(8,128)(2,1)} fusion(bf16[2048,3200]{1,0:T(8,128)(2,1)} %convolution_convert_fusion, f32[2048,3200]{1,0:T(8,128)} %fusion.42, bf16[1,2048,640]{1,2,0:T(8,128)(2,1)S(1)} %copy-done.1, f32[2048]{0:T(1024)S(1)} %copy-done.15), kind=kOutput, calls=%fused_computation.32 | convolution fusion | flops 8440463360 | bytes 46047232 | tf_op jit(solution)/shard_map/dot_general | solution.py:10
  259.1 16.0 %convolution_convert_fusion.4 = bf16[640,3200]{1,0:T(8,128)(2,1)} fusion(bf16[2048,3200]{1,0:T(8,128)(2,1)} %get-tuple-element.10, bf16[2048,640]{0,1:T(8,128)(2,1)} %copy-done.10, f32[2048]{0:T(1024)S(1)} %fusion.114), kind=kOutput, calls=%fused_computation.36 | convolution fusion | flops 8394588160 | bytes 19832832 | tf_op jit(solution)/shard_map/dot_general | solution.py:10
  275.2 0.1 reduce-scatter.7.cloned.1.call-start
  275.3 27.1 %fusion.13 = bf16[640,3200]{1,0:T(8,128)(2,1)} fusion(f32[2048,3200]{1,0:T(8,128)} %get-tuple-element.36, bf16[2048,3200]{1,0:T(8,128)(2,1)} %convolution_convert_fusion, f32[2048,3200]{1,0:T(8,128)} %fusion.42, bf16[1,2048,640]{1,2,0:T(8,128)(2,1)S(1)} %copy-done.1, f32[2048]{0:T(1024)S(1)} %copy-done.15), kind=kOutput, calls=%fused_computation.31 | convolution fusion | flops 8466677760 | bytes 72261632 | tf_op jit(solution)/shard_map/dot_general | solution.py:10
  302.5 5.8 fusion.127
  308.3 5.0 fusion.92
  313.4 0.7 all-gather.17.cloned.1.call-update
  314.2 5.8 fusion.128
  320.0 5.2 reduce-scatter.11.cloned.1.call-done
  325.2 5.6 fusion.86
  330.9 0.6 all-gather.13.cloned.1.call-update
  331.6 5.8 fusion.129
  337.4 22.7 %reduce-scatter.9.cloned.1.call-done = bf16[80,3200]{1,0:T(8,128)(2,1)} async-done(((bf16[640,3200]{1,0:T(8,128)(2,1)}), bf16[80,3200]{1,0:T(8,128)(2,1)}) %reduce-scatter.9.cloned.1.call-update) | async-done | bytes 512016 | tf_op jit(solution)/shard_map/reduce_scatter | solution.py:60
  360.0 35.4 %reduce-scatter.7.cloned.1.call-done = bf16[80,3200]{1,0:T(8,128)(2,1)} async-done(((bf16[640,3200]{1,0:T(8,128)(2,1)}), bf16[80,3200]{1,0:T(8,128)(2,1)}) %reduce-scatter.7.cloned.1.call-update) | async-done | bytes 512016 | tf_op jit(solution)/shard_map/reduce_scatter | solution.py:60
  395.4 5.6 fusion.80
  401.0 0.2 all-gather.9.cloned.1.call-start
  401.3 0.4 all-gather.9.cloned.1.call-update
  401.7 3.6 pad_maximum_fusion.5
  405.4 2.4 pad_maximum_fusion.4
  407.8 0.9 copy-done.8
  408.6 0.3 copy-done.9
  409.0 2.2 pad_maximum_fusion.3
  411.2 15.3 %all-gather.15.cloned.1.call-done = bf16[3200,640]{1,0:T(8,128)(2,1)} async-done(((bf16[400,640]{1,0:T(8,128)(2,1)}), bf16[3200,640]{1,0:T(8,128)(2,1)}) %all-gather.15.cloned.1.call-update) | async-done | bytes 4096016 | tf_op jit(solution)/shard_map/all_gather | solution.py:64
  426.5 28.8 %all-gather.17.cloned.1.call-done = bf16[3200,640]{1,0:T(8,128)(2,1)} async-done(((bf16[400,640]{1,0:T(8,128)(2,1)}), bf16[3200,640]{1,0:T(8,128)(2,1)}) %all-gather.17.cloned.1.call-update) | async-done | bytes 4096016 | tf_op jit(solution)/shard_map/all_gather | solution.py:64
  455.4 7.6 %pad_maximum_fusion.2 = bf16[2,3200,640]{2,1,0:T(8,128)(2,1)} fusion(bf16[1,3200,640]{2,1,0:T(8,128)(2,1)} %bitcast.193, bf16[1,3200,640]{2,1,0:T(8,128)(2,1)} %bitcast.192), kind=kLoop, calls=%fused_computation.27 | loop fusion | flops 4096000 | bytes 16384000 | tf_op jit(solution)/shard_map/stack | solution.py:79
  462.9 21.3 %all-gather.11.cloned.1.call-done = bf16[640,3200]{1,0:T(8,128)(2,1)} async-done(((bf16[80,3200]{1,0:T(8,128)(2,1)}), bf16[640,3200]{1,0:T(8,128)(2,1)}) %all-gather.11.cloned.1.call-update) | async-done | bytes 4096016 | tf_op jit(solution)/shard_map/all_gather | solution.py:64
  484.2 28.7 %all-gather.13.cloned.1.call-done = bf16[640,3200]{1,0:T(8,128)(2,1)} async-done(((bf16[80,3200]{1,0:T(8,128)(2,1)}), bf16[640,3200]{1,0:T(8,128)(2,1)}) %all-gather.13.cloned.1.call-update) | async-done | bytes 4096016 | tf_op jit(solution)/shard_map/all_gather | solution.py:64
  512.9 7.6 %pad_maximum_fusion.1 = bf16[2,640,3200]{2,1,0:T(8,128)(2,1)} fusion(bf16[1,640,3200]{2,1,0:T(8,128)(2,1)} %bitcast.195, bf16[1,640,3200]{2,1,0:T(8,128)(2,1)} %bitcast.194), kind=kLoop, calls=%fused_computation.26 | loop fusion | flops 4096000 | bytes 16384000 | tf_op jit(solution)/shard_map/stack | solution.py:79
  520.5 21.3 %all-gather.7.cloned.1.call-done = bf16[640,3200]{1,0:T(8,128)(2,1)} async-done(((bf16[80,3200]{1,0:T(8,128)(2,1)}), bf16[640,3200]{1,0:T(8,128)(2,1)}) %all-gather.7.cloned.1.call-update) | async-done | bytes 4096016 | tf_op jit(solution)/shard_map/all_gather | solution.py:64
  541.8 28.7 %all-gather.9.cloned.1.call-done = bf16[640,3200]{1,0:T(8,128)(2,1)} async-done(((bf16[80,3200]{1,0:T(8,128)(2,1)}), bf16[640,3200]{1,0:T(8,128)(2,1)}) %all-gather.9.cloned.1.call-update) | async-done | bytes 4096016 | tf_op jit(solution)/shard_map/all_gather | solution.py:64
  570.5 7.6 %pad_maximum_fusion = bf16[2,640,3200]{2,1,0:T(8,128)(2,1)} fusion(bf16[1,640,3200]{2,1,0:T(8,128)(2,1)} %bitcast.197, bf16[1,640,3200]{2,1,0:T(8,128)(2,1)} %bitcast.196), kind=kLoop, calls=%fused_computation.25 | loop fusion | flops 4096000 | bytes 16384000 | tf_op jit(solution)/shard_map/stack | solution.py:79
  (54 shorter events, 1.2 us)
Async XLA Ops:
  7.2 301.1 %reduce-scatter.15.cloned.1.call-start = ((), (), s32[]{:S(2)}) async-start(), calls=%async_computation.14 | async-start | bytes 4608000 | tf_op jit(solution)/shard_map/reduce_scatter | solution.py:60
  10.3 47.2 %copy-start = (bf16[1,2048,640]{1,2,0:T(8,128)(2,1)}, bf16[1,2048,640]{1,2,0:T(8,128)(2,1)S(1)}, u32[]{:S(2)}) copy-start(bf16[1,2048,640]{1,2,0:T(8,128)(2,1)S(1)} %copy.20) | copy-start | bytes 7864324
  10.8 18.6 %copy-start.14 = (f32[2048]{0:T(1024)}, f32[2048]{0:T(1024)S(1)}, u32[]{:S(2)}) copy-start(f32[2048]{0:T(1024)S(1)} %add_rsqrt_fusion) | copy-start | bytes 24580
  71.3 17.3 %copy-start.10 = (bf16[2048,640]{0,1:T(8,128)(2,1)}, bf16[2048,640]{0,1:T(8,128)(2,1)S(1)}, u32[]{:S(2)}) copy-start(bf16[2048,640]{0,1:T(8,128)(2,1)S(1)} %get-tuple-element.38) | copy-start | bytes 7864324
  140.2 13.4 %copy-start.11 = (bf16[2048,640]{0,1:T(8,128)(2,1)S(1)}, bf16[2048,640]{0,1:T(8,128)(2,1)}, u32[]{:S(2)}) copy-start(bf16[2048,640]{0,1:T(8,128)(2,1)} %copy-done.10) | copy-start | bytes 7864324
  169.0 1.5 copy-start.13
  186.0 23.2 %copy-start.12 = (bf16[2048,640]{0,1:T(8,128)(2,1)S(1)}, bf16[2048,640]{0,1:T(8,128)(2,1)}, u32[]{:S(2)}) copy-start(bf16[2048,640]{0,1:T(8,128)(2,1)} %copy-done.10) | copy-start | bytes 7864324
  186.0 122.3 %reduce-scatter.17.cloned.1.call-start = ((), (), s32[]{:S(2)}) async-start(), calls=%async_computation.16 | async-start | bytes 4608000 | tf_op jit(solution)/shard_map/reduce_scatter | solution.py:60
  209.1 110.9 %reduce-scatter.13.cloned.1.call-start = ((), (), s32[]{:S(2)}) async-start(), calls=%async_computation.12 | async-start | bytes 4608000 | tf_op jit(solution)/shard_map/reduce_scatter | solution.py:60
  223.4 16.7 %copy-start.1 = (bf16[1,2048,640]{1,2,0:T(8,128)(2,1)S(1)}, bf16[1,2048,640]{1,2,0:T(8,128)(2,1)}, u32[]{:S(2)}) copy-start(bf16[1,2048,640]{1,2,0:T(8,128)(2,1)} %copy-done) | copy-start | bytes 7864324
  223.4 16.7 %copy-start.15 = (f32[2048]{0:T(1024)S(1)}, f32[2048]{0:T(1024)}, u32[]{:S(2)}) copy-start(f32[2048]{0:T(1024)} %copy-done.14) | copy-start | bytes 24580
  223.4 101.8 %reduce-scatter.11.cloned.1.call-start = ((), (), s32[]{:S(2)}) async-start(), calls=%async_computation.10 | async-start | bytes 4608000 | tf_op jit(solution)/shard_map/reduce_scatter | solution.py:60
  259.0 101.0 %reduce-scatter.9.cloned.1.call-start = ((), (), s32[]{:S(2)}) async-start(), calls=%async_computation.8 | async-start | bytes 4608000 | tf_op jit(solution)/shard_map/reduce_scatter | solution.py:60
  275.2 120.2 %reduce-scatter.7.cloned.1.call-start = ((), (), s32[]{:S(2)}) async-start(), calls=%async_computation.6 | async-start | bytes 4608000 | tf_op jit(solution)/shard_map/reduce_scatter | solution.py:60
  302.4 124.1 %all-gather.15.cloned.1.call-start = ((), (), s32[]{:S(2)}) async-start(), calls=%async_computation.15 | async-start | bytes 4608000 | tf_op jit(solution)/shard_map/all_gather | solution.py:64
  313.3 142.0 %all-gather.17.cloned.1.call-start = ((), (), s32[]{:S(2)}) async-start(), calls=%async_computation.17 | async-start | bytes 4608000 | tf_op jit(solution)/shard_map/all_gather | solution.py:64
  314.2 170.1 %all-gather.11.cloned.1.call-start = ((), (), s32[]{:S(2)}) async-start(), calls=%async_computation.11 | async-start | bytes 4608000 | tf_op jit(solution)/shard_map/all_gather | solution.py:64
  330.9 182.0 %all-gather.13.cloned.1.call-start = ((), (), s32[]{:S(2)}) async-start(), calls=%async_computation.13 | async-start | bytes 4608000 | tf_op jit(solution)/shard_map/all_gather | solution.py:64
  331.5 210.3 %all-gather.7.cloned.1.call-start = ((), (), s32[]{:S(2)}) async-start(), calls=%async_computation.7 | async-start | bytes 4608000 | tf_op jit(solution)/shard_map/all_gather | solution.py:64
  401.0 169.4 %all-gather.9.cloned.1.call-start = ((), (), s32[]{:S(2)}) async-start(), calls=%async_computation.9 | async-start | bytes 4608000 | tf_op jit(solution)/shard_map/all_gather | solution.py:64
  401.7 3.7 copy-start.2
  401.7 3.7 copy-start.3
  401.7 3.7 copy-start.4
  401.7 3.7 copy-start.5
  405.3 2.4 copy-start.6
  405.3 2.4 copy-start.7
  405.3 3.3 copy-start.8
  405.3 3.6 copy-start.9
Sparse Core Ops, SparseCore 0:
  186.1 33.7 reduce-scatter.14
  222.2 32.5 reduce-scatter.16
  257.2 32.6 reduce-scatter.12
  292.6 32.5 reduce-scatter.10
  327.4 32.5 reduce-scatter.8
  362.8 32.5 reduce-scatter.6
  397.0 29.4 all-gather.14
  428.1 27.2 all-gather.16
  456.9 27.2 all-gather.10
  485.6 27.2 all-gather.12
  514.5 27.2 all-gather.6
  543.2 27.2 all-gather.8

commit v2 on v1

v2 whole, which is shorter than its diff:
```python
import functools

import jax
import jax.numpy as jnp
from jax import lax
from jax.experimental import pallas as pl
from jax.experimental.pallas import tpu as pltpu
from jax.sharding import PartitionSpec as P

NAMES = ("w_gate", "w_up", "w_down")
BF, F32 = jnp.bfloat16, jnp.float32
TILE = 512
LIMIT = 63_000_000


def dot(a, b, dims):
    return lax.dot_general(a, b, (dims, ((), ())), preferred_element_type=F32)


def normed(wide):
    return (wide * lax.rsqrt(jnp.mean(wide * wide, -1, keepdims=True) + 1e-6)).astype(BF)


def adamw(w, m, v, g):
    m = 0.9 * m + 0.1 * g
    v = 0.95 * v + 0.05 * g * g
    step = m * lax.rsqrt(v + 1e-8) + 0.1 * w
    return (w - 0.02 * step).astype(BF), m, v


def pieces(n, step):
    cuts = list(range(0, n - n % step, step)) + [n] if n % step else list(range(0, n + 1, step))
    if len(cuts) > 2 and cuts[-1] - cuts[-2] < step:
        del cuts[-2]
    return list(zip(cuts, cuts[1:]))


def whole(layer, rows, columns):
    return pl.BlockSpec((None, rows, columns), lambda t: (layer, 0, 0), pipeline_mode=pl.Buffered(1))


def tiles(columns):
    return pl.BlockSpec((TILE, columns), lambda t: (t, 0))


def forward(h, wg, wu, wd, layer):
    tokens, d = h.shape
    ff = wg.shape[-1]

    def kernel(h_ref, wg_ref, wu_ref, wd_ref, o_ref):
        wide = h_ref[...].astype(F32)
        a = normed(wide)
        total = jnp.zeros((TILE, d), F32)
        for lo, hi in pieces(ff, 768):
            gate = jnp.dot(a, wg_ref[:, lo:hi], preferred_element_type=F32)
            up = jnp.dot(a, wu_ref[:, lo:hi], preferred_element_type=F32)
            mid = (gate * jax.nn.sigmoid(gate) * up).astype(BF)
            total += jnp.dot(mid, wd_ref[lo:hi, :], preferred_element_type=F32)
        o_ref[...] = (wide + total.astype(BF).astype(F32)).astype(BF)

    return pl.pallas_call(
        kernel,
        grid=(tokens // TILE,),
        in_specs=[tiles(d), whole(layer, d, ff), whole(layer, d, ff), whole(layer, ff, d)],
        out_specs=tiles(d),
        out_shape=jax.ShapeDtypeStruct((tokens, d), BF),
        compiler_params=pltpu.CompilerParams(vmem_limit_bytes=LIMIT),
        cost_estimate=pl.CostEstimate(flops=6 * tokens * d * ff, bytes_accessed=2 * 3 * d * ff, transcendentals=tokens * ff),
        name="forward",
    )(h, wg, wu, wd)


def middles(h, dy, wg, wu, wd, layer):
    tokens, d = h.shape
    ff = wg.shape[-1]

    def kernel(h_ref, dy_ref, wg_ref, wu_ref, wd_ref, a_ref, o_ref):
        a = normed(h_ref[...].astype(F32))
        a_ref[...] = a
        dy = dy_ref[...]
        for lo, hi in pieces(ff, 768):
            gate = jnp.dot(a, wg_ref[:, lo:hi], preferred_element_type=F32)
            up = jnp.dot(a, wu_ref[:, lo:hi], preferred_element_type=F32)
            s = jax.nn.sigmoid(gate)
            silu = gate * s
            o_ref[2, :, lo:hi] = (silu * up).astype(BF)
            dmid = dot(dy, wd_ref[lo:hi, :], ((1,), (1,))).astype(BF).astype(F32)
            o_ref[0, :, lo:hi] = (dmid * up * (s * (1 + gate * (1 - s)))).astype(BF)
            o_ref[1, :, lo:hi] = (dmid * silu).astype(BF)

    return pl.pallas_call(
        kernel,
        grid=(tokens // TILE,),
        in_specs=[tiles(d), tiles(d), whole(layer, d, ff), whole(layer, d, ff), whole(layer, ff, d)],
        out_specs=[tiles(d), pl.BlockSpec((3, TILE, ff), lambda t: (0, t, 0))],
        out_shape=[jax.ShapeDtypeStruct((tokens, d), BF), jax.ShapeDtypeStruct((3, tokens, ff), BF)],
        compiler_params=pltpu.CompilerParams(vmem_limit_bytes=LIMIT),
        cost_estimate=pl.CostEstimate(flops=6 * tokens * d * ff, bytes_accessed=2 * 3 * (d + tokens) * ff, transcendentals=tokens * ff),
        name="middles",
    )(h, dy, wg, wu, wd)


def by_states(three, h, dy, wg, wu, layer):
    tokens, d = h.shape
    ff = wg.shape[-1]

    def kernel(t_ref, h_ref, dy_ref, wg_ref, wu_ref, o_ref):
        da = dot(t_ref[0], wg_ref[...], ((1,), (1,))).astype(BF) + dot(t_ref[1], wu_ref[...], ((1,), (1,))).astype(BF)
        da = da.astype(F32)
        wide = h_ref[...].astype(F32)
        scale = lax.rsqrt(jnp.mean(wide * wide, -1, keepdims=True) + 1e-6)
        inner = jnp.mean(da * wide, -1, keepdims=True)
        back = (da * scale - wide * (inner * scale * scale * scale)).astype(BF)
        o_ref[...] = (dy_ref[...].astype(F32) + back.astype(F32)).astype(BF)

    return pl.pallas_call(
        kernel,
        grid=(tokens // TILE,),
        in_specs=[pl.BlockSpec((2, TILE, ff), lambda t: (0, t, 0)), tiles(d), tiles(d), whole(layer, d, ff), whole(layer, d, ff)],
        out_specs=tiles(d),
        out_shape=jax.ShapeDtypeStruct((tokens, d), BF),
        compiler_params=pltpu.CompilerParams(vmem_limit_bytes=LIMIT),
        cost_estimate=pl.CostEstimate(flops=4 * tokens * d * ff, bytes_accessed=4 * (d + tokens) * ff, transcendentals=0),
        name="by_states",
    )(three, h, dy, wg, wu)


def summed(a, dy, three, size, collective_id):
    tokens, d = a.shape
    ff = three.shape[-1]
    chips, rows = size // 2, d // size
    assert chips == 4 and ff % d == 0 and ff // size % rows == 0 and d % size == 0
    cuts = ff // d
    blocks = 3 * cuts
    first = 48
    halves = (pl.ds(0, first), pl.ds(first, rows - first))
    late = cuts - 1
    lag0, lag1, lag2, lag3 = 1, 2, 4, 6
    steps = blocks + late + lag3

    def kernel(a_ref, dy_ref, t_ref, g_ref, u_ref, d_ref, own, near, out_a, out_b, in_a, in_b, send, recv):
        t = pl.program_id(0)
        me = lax.axis_index("dp")
        chip, core = me // 2, me % 2

        def at(step):
            return lax.rem(chip + step + chips, chips)

        def device(step):
            return {"dp": at(step) * 2 + core}

        def copy(src, dst, kind, q, to):
            return pltpu.make_async_remote_copy(
                src_ref=src, dst_ref=dst, send_sem=send.at[kind, q], recv_sem=recv.at[kind, q], device_id=to, device_id_type=pl.DeviceIdType.MESH
            )

        def way(q):
            return 1 - 2 * lax.rem(q, 2)

        def over(q):
            return copy(own.at[q, :, 1 - core], near.at[q], 0, q, {"dp": me + 1 - 2 * core})

        def message(q, kind, second):
            to = device(-way(q) if second == (kind != 1) else way(q))
            out, into = (out_b, in_b) if second else (out_a, in_a)
            return copy(out.at[q, kind], into.at[q, kind], 1 + 2 * kind + second, q, to)

        def part(q, c, half):
            return own[q, c, core, half, :].astype(F32) + near[q, c, half, :].astype(F32)

        def when(lag, f):
            e = t - lag
            on = jnp.logical_and(e >= 0, jnp.logical_or(e < 2 * cuts, jnp.logical_and(e >= 2 * cuts + late, e < blocks + late)))
            pl.when(on)(lambda: f(jnp.where(e < 2 * cuts, e, e - late)))

        @pl.when(t == 0)
        def _():
            barrier = pltpu.get_barrier_semaphore()
            for to in ({"dp": me + 1 - 2 * core}, device(1), device(-1)):
                pl.semaphore_signal(barrier, inc=1, device_id=to, device_id_type=pl.DeviceIdType.MESH)
            pl.semaphore_wait(barrier, 3)

        def finish(q):
            for kind in range(3):
                for second in (0, 1):
                    if kind:
                        message(q, kind, second).wait_recv()
            for second, into in ((0, in_a), (1, in_b)):
                half = halves[second]
                g = part(q, chip, half) + into[q, 1].astype(F32) + into[q, 2].astype(F32)
                g = g.astype(BF)
                at_column = pl.ds(pl.multiple_of(lax.rem(q, cuts) * d, 128), d)
                at_row = pl.ds(pl.multiple_of(lax.rem(q, cuts) * rows + half.start, 16), half.size)

                @pl.when(q < cuts)
                def _():
                    g_ref[half, at_column] = g

                @pl.when(jnp.logical_and(q >= cuts, q < 2 * cuts))
                def _():
                    u_ref[half, at_column] = g

                @pl.when(q >= 2 * cuts)
                def _():
                    d_ref[at_row, :] = g

            over(q).wait_send()
            for kind in range(3):
                for second in (0, 1):
                    message(q, kind, second).wait_send()

        def join(q):
            for second, out, into in ((0, out_a, in_a), (1, out_b, in_b)):
                message(q, 0, second).wait_recv()
                c = at(way(q) if second == 0 else -way(q))
                out[q, 2] = (part(q, c, halves[second]) + into[q, 0].astype(F32)).astype(BF)
            for second in (0, 1):
                message(q, 2, second).start()

        def split(q):
            over(q).wait_recv()
            for second, out in ((0, out_a), (1, out_b)):
                out[q, 0] = part(q, at(2), halves[second]).astype(BF)
                c = at(-way(q) if second == 0 else way(q))
                out[q, 1] = part(q, c, halves[second]).astype(BF)
            for kind in (0, 1):
                for second in (0, 1):
                    message(q, kind, second).start()

        when(lag0, lambda q: over(q).start())
        when(lag2, join)
        when(lag1, split)
        when(lag3, finish)

        @pl.when(t < 2 * cuts)
        def _():
            g = dot(a_ref[...], t_ref[...], ((0,), (0,))).astype(BF)
            own[t] = g.reshape(chips, 2, rows, d)

        @pl.when(jnp.logical_and(t >= 2 * cuts, t < blocks))
        def _():
            g = dot(t_ref[...], dy_ref[...], ((0,), (0,))).astype(BF)
            for p in range(size):
                n = (t - 2 * cuts) * size + p
                dev = n // cuts
                own[2 * cuts + lax.rem(n, cuts), dev // 2, lax.rem(dev, 2)] = g[p * rows : (p + 1) * rows]

    def block(t):
        t = jnp.minimum(t, blocks - 1)
        return t // cuts, 0, lax.rem(t, cuts)

    once = functools.partial(pl.BlockSpec, index_map=lambda t: (0, 0), pipeline_mode=pl.Buffered(1))
    second = rows - first
    return pl.pallas_call(
        kernel,
        grid=(steps,),
        in_specs=[once((tokens, d)), once((tokens, d)), pl.BlockSpec((None, tokens, d), block)],
        out_specs=[pl.BlockSpec((rows, ff), lambda t: (0, 0))] * 2 + [pl.BlockSpec((ff // size, d), lambda t: (0, 0))],
        out_shape=[jax.ShapeDtypeStruct((rows, ff), BF)] * 2 + [jax.ShapeDtypeStruct((ff // size, d), BF)],
        scratch_shapes=[
            pltpu.VMEM((blocks, chips, 2, rows, d), BF),
            pltpu.VMEM((blocks, chips, rows, d), BF),
            pltpu.VMEM((blocks, 3, first, d), BF),
            pltpu.VMEM((blocks, 3, second, d), BF),
            pltpu.VMEM((blocks, 3, first, d), BF),
            pltpu.VMEM((blocks, 3, second, d), BF),
            pltpu.SemaphoreType.DMA((7, blocks)),
            pltpu.SemaphoreType.DMA((7, blocks)),
        ],
        compiler_params=pltpu.CompilerParams(vmem_limit_bytes=LIMIT, collective_id=collective_id, has_side_effects=True),
        cost_estimate=pl.CostEstimate(flops=6 * tokens * d * ff, bytes_accessed=2 * 3 * tokens * ff, transcendentals=0),
        name="summed",
    )(a, dy, three)


def solution(mesh):
    size = mesh.shape["dp"]

    def body(x, dy, *arrays):
        weights, ms, vs = (dict(zip(NAMES, arrays[i : i + 3])) for i in (0, 3, 6))
        wg, wu, wd = (weights[k] for k in NAMES)
        states, d = [x[0]], dy[0]
        layers = wg.shape[0]
        me = lax.axis_index("dp")
        for n in range(layers - 1):
            states.append(forward(states[-1], wg, wu, wd, n))
        new = {}
        for n in reversed(range(layers)):
            a, three = middles(states[n], d, wg, wu, wd, n)
            sums = summed(a, d, three, size, n)
            if n:
                three, sums = lax.optimization_barrier((three, sums))
                d = by_states(three, states[n], d, wg, wu, n)
            for k, g in zip(NAMES, sums):
                rows = g.shape[0]
                w = lax.dynamic_slice_in_dim(weights[k][n], me * rows, rows, 0)
                w, m, v = adamw(w.astype(F32), ms[k][n], vs[k][n], g.astype(F32))
                new[k, n] = lax.all_gather(w, "dp", axis=0, tiled=True), m, v
        return tuple(jnp.stack([new[k, n][i] for n in range(layers)]) for i in range(3) for k in NAMES)

    rows = P(None, "dp", None)
    seqs = P(("rep", "dp"), None, None)
    return jax.shard_map(
        body,
        mesh=mesh,
        in_specs=(seqs, seqs, P(), P(), P()) + (rows,) * 6,
        out_specs=(P("rep", None, None),) * 3 + (P("rep", "dp", None),) * 6,
        check_vma=False,
    )
```

time: 592 us -> 516 us (0.87)
  Pallas kernels: 0 us -> 304 us
  matrix products: 284 us -> 0 us
  waiting for transfers between devices: 210 us -> 133 us
  local copies, waits for them, and re-layouts: 26.1 us -> 16.7 us
  other arithmetic: 49.5 us -> 41.7 us
    pallas_call x0 -> x6, Pallas kernels: none -> 304 us  [the longest x2 145 us: summed(): pl.pallas_call(kernel, grid=(steps,), in_specs=[once((tokens, d)), once((...]
    dot_general x15 -> x0, matrix products: 284 us -> none  [dot(): lax.dot_general(a, b, (dims, ((), ())), preferred_element_type=jnp.float32)]
    reduce_scatter x6 -> x0, waiting for transfers between devices: 63.2 us -> none  [finish(): lax.psum_scatter(g.astype(jnp.bfloat16), 'dp', scatter_dimension=0, tiled...]
    all_gather x6, waiting for transfers between devices: 144 us -> 131 us  [body(): new[k, n] = (lax.all_gather(w, 'dp', axis=0, tiled=True), m, v)]
  transfers between devices with their start and end apart: 12 -> 6, of which waited for: 9 -> 6; matrix products, arithmetic and copies ran while one was open for 30% -> 7% of each run, Pallas kernels for 0% -> 0%
where the time goes in v2:
time: 516 us; the launch traced here: 510 us
  Pallas kernels  304 us (59%)
  waiting for transfers between devices  133 us (26%)
  other arithmetic  41.7 us (8%)
  local copies, waits for them, and re-layouts  16.7 us (3%)
  between operations  14.6 us (3%)
    pallas_call x2, Pallas kernels, summed(): pl.pallas_call(kernel, grid=(steps,), in_specs=[once((tokens, d)), once((...  145 us
    all_gather x6, waiting for transfers between devices, body(): new[k, n] = (lax.all_gather(w, 'dp', axis=0, tiled=True), m, v)  131 us
    pallas_call x2, Pallas kernels, middles(): pl.pallas_call(kernel, grid=(tokens // TILE,), in_specs=[tiles(d), tiles(...  90.1 us
    pallas_call x1, Pallas kernels, forward(): pl.pallas_call(kernel, grid=(tokens // TILE,), in_specs=[tiles(d), whole(...  38.4 us
    another operation x6, other arithmetic, body(): jnp.stack([new[k, n][i] for n in range(layers)])  30.9 us
    pallas_call x1, Pallas kernels, by_states(): pl.pallas_call(kernel, grid=(tokens // TILE,), in_specs=[pl.BlockSpec((2,...  29.7 us
    slice x3, local copies, waits for them, and re-layouts, body(): w = lax.dynamic_slice_in_dim(weights[k][n], me * rows, rows, 0)  13.6 us
    convert_element_type x3, other arithmetic, adamw(): return ((w - 0.02 * step).astype(BF), m, v)  10.8 us
  transfers between devices with their start and end apart: 6, of which 6 were waited for; matrix products, arithmetic and copies ran while one was open for 7% of the time, Pallas kernels for 0%

profile of v2, /device:TPU:113, one launch (start us, length us, event | category | flops | bytes accessed | tf_op | source)
XLA Modules:
  0.0 509.9 jit_solution(13309529117894395781)
XLA Ops:
  7.2 0.1 all-gather.15.cloned.1.call-start
  7.3 5.9 %fusion.42 = (bf16[1,3200,640]{2,1,0:T(8,128)(2,1)}, bf16[1,3200,640]{2,1,0:T(8,128)(2,1)}) fusion(bf16[2,3200,640]{2,1,0:T(8,128)(2,1)} %wd_ref.5), kind=kLoop, calls=%fused_computation.75 | loop fusion | bytes 16384000 | tf_op jit(solution)/shard_map/slice | solution.py:296
  13.1 38.4 %forward.1.h_ref = bf16[2048,640]{1,0:T(8,128)(2,1)} custom-call(bf16[2048,640]{1,0:T(8,128)(2,1)} %bitcast.131, bf16[2,640,3200]{2,1,0:T(8,128)(2,1)} %wg_ref.7, bf16[2,640,3200]{2,1,0:T(8,128)(2,1)} %wu_ref.7, bf16[2,3200,640]{2,1,0:T(8,128)(2,1)} %wd_ref.5), custom_call_target="tpu_custom_call" | custom-call | flops 25165824000 | bytes 12288000 | tf_op jit(solution)/shard_map/forward/pallas_call | solution.py:61
  51.5 45.3 %middles.2 = (bf16[2048,640]{1,0:T(8,128)(2,1)}, bf16[3,2048,3200]{2,1,0:T(8,128)(2,1)}) custom-call(bf16[2048,640]{1,0:T(8,128)(2,1)} %forward.1.h_ref, bf16[2048,640]{1,0:T(8,128)(2,1)} %bitcast.128, bf16[2,640,3200]{2,1,0:T(8,128)(2,1)} %wg_ref.7, bf16[2,640,3200]{2,1,0:T(8,128)(2,1)} %wu_ref.7, bf16[2,3200,640]{2,1,0:T(8,128)(2,1)} %wd_ref.5), custom_call_target="tpu_custom_call" | custom-call | flops 25165824000 | bytes 51609600 | tf_op jit(solution)/shard_map/middles/pallas_call | solution.py:91
  96.8 73.6 %summed.2 = (bf16[80,3200]{1,0:T(8,128)(2,1)}, bf16[80,3200]{1,0:T(8,128)(2,1)}, bf16[400,640]{1,0:T(8,128)(2,1)}) custom-call(bf16[2048,640]{1,0:T(8,128)(2,1)} %get-tuple-element.24.a_ref, bf16[2048,640]{1,0:T(8,128)(2,1)} %bitcast.129, bf16[3,2048,3200]{2,1,0:T(8,128)(2,1)} %get-tuple-element.28.t_ref), custom_call_target="tpu_custom_call" | custom-call | flops 25165824000 | bytes 39321600 | tf_op jit(solution)/shard_map/summed/pallas_call | solution.py:254
  170.4 29.7 %by_states.1.dy_ref = bf16[2048,640]{1,0:T(8,128)(2,1)} custom-call(bf16[3,2048,3200]{2,1,0:T(8,128)(2,1)} %get-tuple-element.28.t_ref, bf16[2048,640]{1,0:T(8,128)(2,1)} %forward.1.h_ref, bf16[2048,640]{1,0:T(8,128)(2,1)} %bitcast.130, bf16[2,640,3200]{2,1,0:T(8,128)(2,1)} %wg_ref.7, bf16[2,640,3200]{2,1,0:T(8,128)(2,1)} %wu_ref.7), custom_call_target="tpu_custom_call" | custom-call | flops 16777216000 | bytes 34406400 | tf_op jit(solution)/shard_map/by_states/pallas_call | solution.py:116
  200.0 44.8 %middles.3 = (bf16[2048,640]{1,0:T(8,128)(2,1)}, bf16[3,2048,3200]{2,1,0:T(8,128)(2,1)}) custom-call(bf16[2048,640]{1,0:T(8,128)(2,1)} %bitcast.132, bf16[2048,640]{1,0:T(8,128)(2,1)} %by_states.1.dy_ref, bf16[2,640,3200]{2,1,0:T(8,128)(2,1)} %wg_ref.7, bf16[2,640,3200]{2,1,0:T(8,128)(2,1)} %wu_ref.7, bf16[2,3200,640]{2,1,0:T(8,128)(2,1)} %wd_ref.5), custom_call_target="tpu_custom_call" | custom-call | flops 25165824000 | bytes 51609600 | tf_op jit(solution)/shard_map/middles/pallas_call | solution.py:91
  244.9 71.8 %summed.3 = (bf16[80,3200]{1,0:T(8,128)(2,1)}, bf16[80,3200]{1,0:T(8,128)(2,1)}, bf16[400,640]{1,0:T(8,128)(2,1)}) custom-call(bf16[2048,640]{1,0:T(8,128)(2,1)} %get-tuple-element.29.a_ref, bf16[2048,640]{1,0:T(8,128)(2,1)} %by_states.1.dy_ref, bf16[3,2048,3200]{2,1,0:T(8,128)(2,1)} %get-tuple-element.30.t_ref), custom_call_target="tpu_custom_call" | custom-call | flops 25165824000 | bytes 39321600 | tf_op jit(solution)/shard_map/summed/pallas_call | solution.py:254
  316.7 5.1 fusion.20
  321.8 0.1 all-gather.15.cloned.1.call-update
  321.8 0.1 all-gather.17.cloned.1.call-start
  321.9 0.7 all-gather.17.cloned.1.call-update
  322.6 0.1 all-gather.11.cloned.1.call-start
  322.7 0.0 copy-start.8
  322.7 0.0 copy-start.9
  322.8 3.9 fusion.43
  326.6 0.1 copy-done.8
  326.7 0.6 copy-done.9
  327.3 0.1 copy-done.14
  327.4 0.2 copy-done.15
  327.5 2.9 fusion.14
  330.4 0.1 all-gather.11.cloned.1.call-update
  330.5 0.1 all-gather.13.cloned.1.call-start
  330.6 0.6 all-gather.13.cloned.1.call-update
  331.1 0.1 all-gather.9.cloned.1.call-start
  331.2 3.9 fusion.44
  335.1 0.1 copy-done.10
  335.2 0.6 copy-done.11
  335.8 0.1 copy-done.12
  335.9 0.2 copy-done.13
  336.0 2.9 fusion.8
  338.9 0.1 all-gather.9.cloned.1.call-update
  339.0 0.1 all-gather.7.cloned.1.call-start
  339.1 0.6 all-gather.7.cloned.1.call-update
  339.7 3.6 pad_maximum_fusion.5
  343.3 2.4 pad_maximum_fusion.4
  345.7 0.9 copy-done.6
  346.6 0.3 copy-done.7
  346.9 2.2 pad_maximum_fusion.3
  349.2 2.3 all-gather.15.cloned.1.call-done
  351.5 28.8 %all-gather.17.cloned.1.call-done = bf16[3200,640]{1,0:T(8,128)(2,1)} async-done(((bf16[400,640]{1,0:T(8,128)(2,1)}), bf16[3200,640]{1,0:T(8,128)(2,1)}) %all-gather.17.cloned.1.call-update) | async-done | bytes 4096016 | tf_op jit(solution)/shard_map/all_gather | solution.py:298
  380.3 7.6 %pad_maximum_fusion.2 = bf16[2,3200,640]{2,1,0:T(8,128)(2,1)} fusion(bf16[1,3200,640]{2,1,0:T(8,128)(2,1)} %bitcast.123, bf16[1,3200,640]{2,1,0:T(8,128)(2,1)} %bitcast.122), kind=kLoop, calls=%fused_computation.2 | loop fusion | flops 4096000 | bytes 16384000 | tf_op jit(solution)/shard_map/stack | solution.py:299
  387.9 21.3 %all-gather.11.cloned.1.call-done = bf16[640,3200]{1,0:T(8,128)(2,1)} async-done(((bf16[80,3200]{1,0:T(8,128)(2,1)}), bf16[640,3200]{1,0:T(8,128)(2,1)}) %all-gather.11.cloned.1.call-update) | async-done | bytes 4096016 | tf_op jit(solution)/shard_map/all_gather | solution.py:298
  409.2 28.7 %all-gather.13.cloned.1.call-done = bf16[640,3200]{1,0:T(8,128)(2,1)} async-done(((bf16[80,3200]{1,0:T(8,128)(2,1)}), bf16[640,3200]{1,0:T(8,128)(2,1)}) %all-gather.13.cloned.1.call-update) | async-done | bytes 4096016 | tf_op jit(solution)/shard_map/all_gather | solution.py:298
  437.9 7.6 %pad_maximum_fusion.1 = bf16[2,640,3200]{2,1,0:T(8,128)(2,1)} fusion(bf16[1,640,3200]{2,1,0:T(8,128)(2,1)} %bitcast.125, bf16[1,640,3200]{2,1,0:T(8,128)(2,1)} %bitcast.124), kind=kLoop, calls=%fused_computation.1 | loop fusion | flops 4096000 | bytes 16384000 | tf_op jit(solution)/shard_map/stack | solution.py:299
  445.5 21.1 %all-gather.9.cloned.1.call-done = bf16[640,3200]{1,0:T(8,128)(2,1)} async-done(((bf16[80,3200]{1,0:T(8,128)(2,1)}), bf16[640,3200]{1,0:T(8,128)(2,1)}) %all-gather.9.cloned.1.call-update) | async-done | bytes 4096016 | tf_op jit(solution)/shard_map/all_gather | solution.py:298
  466.6 28.7 %all-gather.7.cloned.1.call-done = bf16[640,3200]{1,0:T(8,128)(2,1)} async-done(((bf16[80,3200]{1,0:T(8,128)(2,1)}), bf16[640,3200]{1,0:T(8,128)(2,1)}) %all-gather.7.cloned.1.call-update) | async-done | bytes 4096016 | tf_op jit(solution)/shard_map/all_gather | solution.py:298
  495.3 7.6 %pad_maximum_fusion = bf16[2,640,3200]{2,1,0:T(8,128)(2,1)} fusion(bf16[1,640,3200]{2,1,0:T(8,128)(2,1)} %bitcast.126, bf16[1,640,3200]{2,1,0:T(8,128)(2,1)} %bitcast.127), kind=kLoop, calls=%fused_computation | loop fusion | flops 4096000 | bytes 16384000 | tf_op jit(solution)/shard_map/stack | solution.py:299
  (20 shorter events, 0.1 us)
Async XLA Ops:
  7.2 344.3 %all-gather.15.cloned.1.call-start = ((), (), s32[]{:S(2)}) async-start(), calls=%async_computation.4 | async-start | bytes 4608000 | tf_op jit(solution)/shard_map/all_gather | solution.py:298
  321.8 58.5 %all-gather.17.cloned.1.call-start = ((), (), s32[]{:S(2)}) async-start(), calls=%async_computation.5 | async-start | bytes 4608000 | tf_op jit(solution)/shard_map/all_gather | solution.py:298
  322.6 86.6 %all-gather.11.cloned.1.call-start = ((), (), s32[]{:S(2)}) async-start(), calls=%async_computation.2 | async-start | bytes 4608000 | tf_op jit(solution)/shard_map/all_gather | solution.py:298
  322.7 4.0 copy-start.8
  322.7 4.6 copy-start.9
  322.7 4.7 copy-start.14
  322.7 4.8 copy-start.15
  330.5 107.4 %all-gather.13.cloned.1.call-start = ((), (), s32[]{:S(2)}) async-start(), calls=%async_computation.3 | async-start | bytes 4608000 | tf_op jit(solution)/shard_map/all_gather | solution.py:298
  331.1 135.5 %all-gather.9.cloned.1.call-start = ((), (), s32[]{:S(2)}) async-start(), calls=%async_computation.1 | async-start | bytes 4608000 | tf_op jit(solution)/shard_map/all_gather | solution.py:298
  331.2 4.0 copy-start.10
  331.2 4.6 copy-start.11
  331.2 4.7 copy-start.12
  331.2 4.8 copy-start.13
  339.0 156.3 %all-gather.7.cloned.1.call-start = ((), (), s32[]{:S(2)}) async-start(), calls=%async_computation | async-start | bytes 4608000 | tf_op jit(solution)/shard_map/all_gather | solution.py:298
  339.6 3.7 copy-start
  339.6 3.6 copy-start.1
  339.6 3.6 copy-start.2
  339.7 3.6 copy-start.3
  343.3 2.4 copy-start.4
  343.3 2.4 copy-start.5
  343.3 3.3 copy-start.6
  343.3 3.6 copy-start.7
Sparse Core Ops, SparseCore 0:
  321.9 29.5 all-gather.14
  353.1 27.2 all-gather.16
  381.9 27.2 all-gather.10
  410.6 27.2 all-gather.12
  439.3 27.2 all-gather.8
  468.0 27.2 all-gather.6

commit v3 on v2

v3 whole, which is shorter than its diff:
```python
import functools

import jax
import jax.numpy as jnp
from jax import lax
from jax.experimental import pallas as pl
from jax.experimental.pallas import tpu as pltpu
from jax.sharding import PartitionSpec as P

NAMES = ("w_gate", "w_up", "w_down")
BF, F32 = jnp.bfloat16, jnp.float32
TILE = 512
LIMIT = 66_900_000


def dot(a, b, dims):
    return lax.dot_general(a, b, (dims, ((), ())), preferred_element_type=F32)


def normed(wide):
    return (wide * lax.rsqrt(jnp.mean(wide * wide, -1, keepdims=True) + 1e-6)).astype(BF)


def adamw(w, m, v, g):
    m = 0.9 * m + 0.1 * g
    v = 0.95 * v + 0.05 * g * g
    step = m * lax.rsqrt(v + 1e-8) + 0.1 * w
    return (w - 0.02 * step).astype(BF), m, v


def pieces(n, step):
    cuts = list(range(0, n - n % step, step)) + [n] if n % step else list(range(0, n + 1, step))
    if len(cuts) > 2 and cuts[-1] - cuts[-2] < step:
        del cuts[-2]
    return list(zip(cuts, cuts[1:]))


def whole(layer, rows, columns):
    return pl.BlockSpec((None, rows, columns), lambda t: (layer, 0, 0), pipeline_mode=pl.Buffered(1))


def tiles(columns):
    return pl.BlockSpec((TILE, columns), lambda t: (t, 0))


def forward(h, wg, wu, wd, layer):
    tokens, d = h.shape
    ff = wg.shape[-1]

    def kernel(h_ref, wg_ref, wu_ref, wd_ref, o_ref):
        wide = h_ref[...].astype(F32)
        a = normed(wide)
        total = jnp.zeros((TILE, d), F32)
        for lo, hi in pieces(ff, 768):
            gate = jnp.dot(a, wg_ref[:, lo:hi], preferred_element_type=F32)
            up = jnp.dot(a, wu_ref[:, lo:hi], preferred_element_type=F32)
            mid = (gate * jax.nn.sigmoid(gate) * up).astype(BF)
            total += jnp.dot(mid, wd_ref[lo:hi, :], preferred_element_type=F32)
        o_ref[...] = (wide + total.astype(BF).astype(F32)).astype(BF)

    return pl.pallas_call(
        kernel,
        grid=(tokens // TILE,),
        in_specs=[tiles(d), whole(layer, d, ff), whole(layer, d, ff), whole(layer, ff, d)],
        out_specs=tiles(d),
        out_shape=jax.ShapeDtypeStruct((tokens, d), BF),
        compiler_params=pltpu.CompilerParams(vmem_limit_bytes=LIMIT),
        cost_estimate=pl.CostEstimate(flops=6 * tokens * d * ff, bytes_accessed=2 * 3 * d * ff, transcendentals=tokens * ff),
        name="forward",
    )(h, wg, wu, wd)


def by_states(three, h, dy, wg, wu, layer):
    tokens, d = h.shape
    ff = wg.shape[-1]

    def kernel(t_ref, h_ref, dy_ref, wg_ref, wu_ref, o_ref):
        da = dot(t_ref[0], wg_ref[...], ((1,), (1,))).astype(BF) + dot(t_ref[1], wu_ref[...], ((1,), (1,))).astype(BF)
        da = da.astype(F32)
        wide = h_ref[...].astype(F32)
        scale = lax.rsqrt(jnp.mean(wide * wide, -1, keepdims=True) + 1e-6)
        inner = jnp.mean(da * wide, -1, keepdims=True)
        back = (da * scale - wide * (inner * scale * scale * scale)).astype(BF)
        o_ref[...] = (dy_ref[...].astype(F32) + back.astype(F32)).astype(BF)

    return pl.pallas_call(
        kernel,
        grid=(tokens // TILE,),
        in_specs=[pl.BlockSpec((2, TILE, ff), lambda t: (0, t, 0)), tiles(d), tiles(d), whole(layer, d, ff), whole(layer, d, ff)],
        out_specs=tiles(d),
        out_shape=jax.ShapeDtypeStruct((tokens, d), BF),
        compiler_params=pltpu.CompilerParams(vmem_limit_bytes=LIMIT),
        cost_estimate=pl.CostEstimate(flops=4 * tokens * d * ff, bytes_accessed=4 * (d + tokens) * ff, transcendentals=0),
        name="by_states",
    )(three, h, dy, wg, wu)


def stepped(h, dy, weights, ms, vs, layer, size, through):
    tokens, d = h.shape
    ff = weights[0].shape[-1]
    chips, rows = size // 2, d // size
    assert chips == 4 and ff % d == 0 and ff // size % rows == 0 and d % size == 0
    cuts = ff // d
    blocks = 3 * cuts
    first = 48
    halves = (pl.ds(0, first), pl.ds(first, rows - first))
    tile = tokens // 4
    per = 7
    made = per * cuts
    lags = (1, 2, 4, 6, 8, 10, 12)
    steps = made + cuts + lags[-1]
    MESH = pl.DeviceIdType.MESH

    def kernel(h_ref, dy_ref, wg_ref, wu_ref, wd_ref, *rest):
        w_hbm, m_hbm, v_hbm = rest[:3], rest[3:6], rest[6:9]
        g_ref, all_ref, two, a_ref, mid, own, near, in_a, in_b, wnew, wold, mold, vold, send, recv, load, keep = rest[9:]
        t = pl.program_id(0)
        me = lax.axis_index("dp")
        chip, core = me // 2, me % 2
        partner = {"dp": me + 1 - 2 * core}

        def at(step):
            return lax.rem(chip + step + chips, chips)

        def dev(step):
            return at(step) * 2 + core

        def copy(src, dst, kind, q, to):
            return pltpu.make_async_remote_copy(
                src_ref=src, dst_ref=dst, send_sem=send.at[kind, q], recv_sem=recv.at[kind, q], device_id=to, device_id_type=MESH
            )

        def way(q):
            return 1 - 2 * lax.rem(q, 2)

        def over(q):
            return copy(own.at[q, :, 1 - core], near.at[q], 0, q, partner)

        def message(q, kind, second):
            step = -way(q) if second == (kind != 1) else way(q)
            c = at(2) if kind == 0 else at(step)
            into = in_b if second else in_a
            return copy(own.at[q, c, core, halves[second], :], into.at[q, kind], 1 + 2 * kind + second, q, {"dp": dev(step)})

        def part(q, c, half):
            return own[q, c, core, half, :].astype(F32) + near[q, c, half, :].astype(F32)

        def there(q, step):
            return copy(wnew.at[q], all_ref.at[q, me], 7 if step == 1 else 8, q, {"dp": dev(step)})

        def onward(q, second):
            step = -way(q) if second else way(q)
            where = all_ref.at[q, dev(-step), halves[second], :]
            return copy(where, where, 9 + second, q, {"dp": dev(step)})

        def across(q, step):
            where = all_ref.at[q, dev(step)]
            return copy(where if step else wnew.at[q], where, 11 + step + (step < 0) * 4, q, partner)

        def kept(q):
            return pltpu.make_async_copy(wnew.at[q], all_ref.at[q, me], keep.at[q])

        def slot(q):
            return jnp.where(q < 2 * cuts, lax.rem(q, 4), q - 2 * cuts + 4)

        def loads(q, which):
            n = slot(q)
            if which < 2:
                columns = pl.ds(pl.multiple_of(q // 2 * d, 128), d)
                mine, ours = (pl.ds(0, rows), columns), (pl.ds(pl.multiple_of(me * rows, 16), rows), columns)
            else:
                b = jnp.maximum(q - 2 * cuts, 0)
                mine = pl.ds(pl.multiple_of(b * rows, 16), rows), pl.ds(0, d)
                ours = pl.ds(pl.multiple_of(me * (ff // size) + b * rows, 16), rows), pl.ds(0, d)
            return (
                pltpu.make_async_copy(w_hbm[which].at[(layer, *ours)], wold.at[n], load.at[n, 0]),
                pltpu.make_async_copy(m_hbm[which].at[(layer, *mine)], mold.at[n], load.at[n, 1]),
                pltpu.make_async_copy(v_hbm[which].at[(layer, *mine)], vold.at[n], load.at[n, 2]),
            )

        @pl.when(t == 0)
        def _():
            barrier = pltpu.get_barrier_semaphore()
            for to in (partner, {"dp": dev(1)}, {"dp": dev(-1)}):
                pl.semaphore_signal(barrier, inc=1, device_id=to, device_id_type=MESH)
            pl.semaphore_wait(barrier, 3)

        def begin(q):
            over(q).start()
            for which, on in enumerate(
                (
                    jnp.logical_and(q < 2 * cuts, lax.rem(q, 2) == 0),
                    jnp.logical_and(q < 2 * cuts, lax.rem(q, 2) == 1),
                    q >= 2 * cuts,
                )
            ):

                @pl.when(on)
                def _(which=which):
                    for one in loads(q, which):
                        one.start()

        def split(q):
            over(q).wait()
            for kind in (0, 1):
                for second in (0, 1):
                    step = -way(q) if second == (kind != 1) else way(q)
                    c = at(2) if kind == 0 else at(step)
                    own[q, c, core, halves[second], :] = part(q, c, halves[second]).astype(BF)
            for kind in (0, 1):
                for second in (0, 1):
                    message(q, kind, second).start()

        def join(q):
            for second, into in ((0, in_a), (1, in_b)):
                message(q, 0, second).wait_recv()
                c = at(-way(q) if second else way(q))
                own[q, c, core, halves[second], :] = (part(q, c, halves[second]) + into[q, 0].astype(F32)).astype(BF)
            for second in (0, 1):
                message(q, 2, second).start()

        def update(q):
            for kind in (1, 2):
                for second in (0, 1):
                    message(q, kind, second).wait_recv()
            for one in loads(q, 2):
                one.wait()
            n = slot(q)
            for second, into in ((0, in_a), (1, in_b)):
                half = halves[second]
                g = (part(q, chip, half) + into[q, 1].astype(F32) + into[q, 2].astype(F32)).astype(BF)
                g_ref[q, half, :] = g
                wnew[q, half, :] = adamw(wold[n, half, :].astype(F32), mold[n, half, :], vold[n, half, :], g.astype(F32))[0]
            there(q, 1).start()
            there(q, -1).start()
            across(q, 0).start()
            kept(q).start()

        def relay(q):
            there(q, 1).wait_recv()
            there(q, -1).wait_recv()
            onward(q, 0).start()
            onward(q, 1).start()
            across(q, 1).start()
            across(q, -1).start()

        def rest_of(q):
            onward(q, 0).wait_recv()
            onward(q, 1).wait_recv()
            across(q, 2).start()

        def close(q):
            for step in (0, 1, -1, 2):
                across(q, step).wait()
            kept(q).wait()
            for kind in range(3):
                for second in (0, 1):
                    message(q, kind, second).wait_send()
            there(q, 1).wait_send()
            there(q, -1).wait_send()
            onward(q, 0).wait_send()
            onward(q, 1).wait_send()

        for lag, act in reversed(tuple(zip(lags, (begin, split, join, update, relay, rest_of, close)))):
            late = t - lag - made + 1
            pl.when(jnp.logical_and(late >= 0, late < cuts))(functools.partial(act, 2 * cuts + late))
            e = t - lag
            r = lax.rem(e, per)
            on = jnp.logical_and(jnp.logical_and(e >= 0, e < made), jnp.logical_and(r >= per - 3, r < per - 1))
            pl.when(on)(functools.partial(act, 2 * (e // per) + r - (per - 3)))

        b, r = t // per, lax.rem(t, per)

        @pl.when(jnp.logical_and(t < made, r < per - 3))
        def _():
            here = pl.ds(pl.multiple_of(r * tile, tile), tile)

            @pl.when(b == 0)
            def _():
                a_ref[here, :] = normed(h_ref[here, :].astype(F32))

            a = a_ref[here, :]
            gate = jnp.dot(a, wg_ref[...], preferred_element_type=F32)
            up = jnp.dot(a, wu_ref[...], preferred_element_type=F32)
            s = jax.nn.sigmoid(gate)
            silu = gate * s
            mid[here, :] = (silu * up).astype(BF)
            dmid = dot(dy_ref[here, :], wd_ref[...], ((1,), (1,))).astype(BF).astype(F32)
            two[0, here, :] = (dmid * up * (s * (1 + gate * (1 - s)))).astype(BF)
            two[1, here, :] = (dmid * silu).astype(BF)

        @pl.when(jnp.logical_and(t < made, jnp.logical_and(r >= per - 3, r < per - 1)))
        def _():
            g = dot(a_ref[...], two[r - (per - 3)], ((0,), (0,))).astype(BF)
            own[2 * b + r - (per - 3)] = g.reshape(chips, 2, rows, d)

        @pl.when(jnp.logical_and(t < made, r == per - 1))
        def _():
            g = dot(mid[...], dy_ref[...], ((0,), (0,))).astype(BF)
            for p in range(size):
                n = b * size + p
                owner = n // cuts
                own[2 * cuts + lax.rem(n, cuts), owner // 2, lax.rem(owner, 2)] = g[p * rows : (p + 1) * rows]

    def block(t):
        return jnp.minimum(t // per, cuts - 1)

    once = functools.partial(pl.BlockSpec, index_map=lambda t: (0, 0), pipeline_mode=pl.Buffered(1))
    wide = pl.BlockSpec((None, d, d), lambda t: (layer, 0, block(t)))
    tall = pl.BlockSpec((None, d, d), lambda t: (layer, block(t), 0))
    hbm = pl.BlockSpec(memory_space=pl.ANY)
    second = rows - first
    two = pl.BlockSpec((2, tokens, d), lambda t: (0, 0, block(t)))
    out_specs = [pl.BlockSpec((blocks, rows, d), lambda t: (0, 0, 0)), hbm]
    out_shape = [jax.ShapeDtypeStruct((blocks, rows, d), BF), jax.ShapeDtypeStruct((blocks, size, rows, d), BF)]
    scratch = [] if through else [pltpu.VMEM((2, tokens, d), BF)]
    return pl.pallas_call(
        kernel,
        grid=(steps,),
        in_specs=[once((tokens, d)), once((tokens, d)), wide, wide, tall] + [hbm] * 9,
        out_specs=out_specs + [two] * through,
        out_shape=out_shape + [jax.ShapeDtypeStruct((2, tokens, ff), BF)] * through,
        scratch_shapes=scratch
        + [
            pltpu.VMEM((tokens, d), BF),
            pltpu.VMEM((tokens, d), BF),
            pltpu.VMEM((blocks, chips, 2, rows, d), BF),
            pltpu.VMEM((blocks, chips, rows, d), BF),
            pltpu.VMEM((blocks, 3, first, d), BF),
            pltpu.VMEM((blocks, 3, second, d), BF),
            pltpu.VMEM((blocks, rows, d), BF),
            pltpu.VMEM((4 + cuts, rows, d), BF),
            pltpu.VMEM((4 + cuts, rows, d), F32),
            pltpu.VMEM((4 + cuts, rows, d), F32),
            pltpu.SemaphoreType.DMA((15, blocks)),
            pltpu.SemaphoreType.DMA((15, blocks)),
            pltpu.SemaphoreType.DMA((4 + cuts, 3)),
            pltpu.SemaphoreType.DMA((blocks,)),
        ],
        compiler_params=pltpu.CompilerParams(vmem_limit_bytes=LIMIT, collective_id=layer, has_side_effects=True),
        cost_estimate=pl.CostEstimate(flops=12 * tokens * d * ff, bytes_accessed=2 * 3 * tokens * ff, transcendentals=0),
        name="stepped",
    )(h, dy, *weights, *weights, *ms, *vs)


def solution(mesh):
    size = mesh.shape["dp"]

    def body(x, dy, *arrays):
        weights, ms, vs = (arrays[i : i + 3] for i in (0, 3, 6))
        wg, wu, wd = weights
        states, d = [x[0]], dy[0]
        layers, width, ff = wg.shape
        rows = width // size
        cuts = ff // width
        me = lax.axis_index("dp")
        for n in range(layers - 1):
            states.append(forward(states[-1], wg, wu, wd, n))
        sums, gathered = [None] * layers, [None] * layers
        for n in reversed(range(layers)):
            sums[n], gathered[n], *two = stepped(states[n], d, weights, ms, vs, n, size, n > 0)
            if n:
                d = by_states(two[0], states[n], d, wg, wu, n)

        def wide(t):
            return jnp.moveaxis(t, 0, -2).reshape(-1, ff)

        def tall(t):
            return jnp.moveaxis(t, 0, -3).reshape(-1, width)

        def each(t):
            return wide(t[0 : 2 * cuts : 2]), wide(t[1 : 2 * cuts : 2]), tall(t[2 * cuts :])

        out = [jnp.stack(one) for one in zip(*map(each, gathered))]
        totals = [jnp.stack(one) for one in zip(*map(each, sums))]
        moments = []
        for w, m, v, g in zip(weights, ms, vs, totals):
            moments.append(adamw(jnp.zeros_like(m), m, v, g.astype(F32))[1:])
        return (*out, *(m for m, _ in moments), *(v for _, v in moments))

    rows = P(None, "dp", None)
    seqs = P(("rep", "dp"), None, None)
    return jax.shard_map(
        body,
        mesh=mesh,
        in_specs=(seqs, seqs, P(), P(), P()) + (rows,) * 6,
        out_specs=(P("rep", None, None),) * 3 + (P("rep", "dp", None),) * 6,
        check_vma=False,
    )
```

time: 516 us -> 509 us (0.986)
  waiting for transfers between devices: 133 us -> 0 us
  local copies, waits for them, and re-layouts: 16.7 us -> 95.5 us
  Pallas kernels: 304 us -> 379 us
  other arithmetic: 41.7 us -> 26.9 us
  between operations: 14.6 us -> 1.2 us
    all_gather x6 -> x0, waiting for transfers between devices: 131 us -> none  [body(): new[k, n] = (lax.all_gather(w, 'dp', axis=0, tiled=True), m, v)]
    pallas_call x4 -> x2, Pallas kernels: 236 us -> 311 us  [stepped(): pl.pallas_call(kernel, grid=(steps,), in_specs=[once((tokens, d)), once((...]
    another operation x0 -> x8, local copies, waits for them, and re-layouts: none -> 45.9 us  [the longest x4 41 us: body(): out = [jnp.stack(one) for one in zip(*map(each, gathered))]]
    transpose x0 -> x12, local copies, waits for them, and re-layouts: none -> 43.5 us  [the longest x8 27.7 us: wide(): return jnp.moveaxis(t, 0, -2).reshape(-1, ff)]
    another operation x6 -> x2, other arithmetic: 30.9 us -> 17.1 us  [body(): out = [jnp.stack(one) for one in zip(*map(each, gathered))]]
    convert_element_type x3 -> x0, other arithmetic: 10.8 us -> none  [adamw(): return ((w - 0.02 * step).astype(BF), m, v)]
    slice x3 -> x2, local copies, waits for them, and re-layouts: 13.6 us -> 3.42 us  [each(): return (wide(t[0:2 * cuts:2]), wide(t[1:2 * cuts:2]), tall(t[2 * cuts:]))]
    add x0 -> x2, other arithmetic: none -> 9.83 us  [adamw(): v = 0.95 * v + 0.05 * g * g]
  transfers between devices with their start and end apart: 6 -> 0, of which waited for: 6 -> 0; matrix products, arithmetic and copies ran while one was open for 7% -> 0% of each run, Pallas kernels for 0% -> 0%
where the time goes in v3:
time: 509 us; the launch traced here: 502 us
  Pallas kernels  379 us (74%)
  local copies, waits for them, and re-layouts  95.5 us (19%)
  other arithmetic  26.9 us (5%)
    pallas_call x2, Pallas kernels, stepped(): pl.pallas_call(kernel, grid=(steps,), in_specs=[once((tokens, d)), once((...  311 us
    another operation x4, local copies, waits for them, and re-layouts, body(): out = [jnp.stack(one) for one in zip(*map(each, gathered))]  41 us
    pallas_call x1, Pallas kernels, forward(): pl.pallas_call(kernel, grid=(tokens // TILE,), in_specs=[tiles(d), whole(...  38.4 us
    pallas_call x1, Pallas kernels, by_states(): pl.pallas_call(kernel, grid=(tokens // TILE,), in_specs=[pl.BlockSpec((2,...  29.6 us
    transpose x8, local copies, waits for them, and re-layouts, wide(): return jnp.moveaxis(t, 0, -2).reshape(-1, ff)  27.7 us
    another operation x2, other arithmetic, body(): out = [jnp.stack(one) for one in zip(*map(each, gathered))]  17.1 us
    transpose x4, local copies, waits for them, and re-layouts, tall(): return jnp.moveaxis(t, 0, -3).reshape(-1, width)  15.8 us

profile of v3, /device:TPU:113, one launch (start us, length us, event | category | flops | bytes accessed | tf_op | source)
XLA Modules:
  0.0 502.3 jit_solution(3345640169077867773)
XLA Ops:
  0.6 38.4 %forward.1.h_ref = bf16[2048,640]{1,0:T(8,128)(2,1)} custom-call(bf16[2048,640]{1,0:T(8,128)(2,1)} %bitcast.32, bf16[2,640,3200]{2,1,0:T(8,128)(2,1)} %rest_0_.3, bf16[2,640,3200]{2,1,0:T(8,128)(2,1)} %rest_1_.3, bf16[2,3200,640]{2,1,0:T(8,128)(2,1)} %rest_2_.3), custom_call_target="tpu_custom_call" | custom-call | flops 25165824000 | bytes 12288000 | tf_op jit(solution)/shard_map/forward/pallas_call | solution.py:61
  39.1 157.9 %stepped.2 = (bf16[15,80,640]{2,1,0:T(8,128)(2,1)}, bf16[15,8,80,640]{3,2,1,0:T(8,128)(2,1)}, bf16[2,2048,3200]{2,1,0:T(8,128)(2,1)}) custom-call(bf16[2048,640]{1,0:T(8,128)(2,1)} %forward.1.h_ref, bf16[2048,640]{1,0:T(8,128)(2,1)} %bitcast.30, bf16[2,640,3200]{2,1,0:T(8,128)(2,1)} %rest_0_.3, bf16[2,640,3200]{2,1,0:T(8,128)(2,1)} %rest_1_.3, ...), custom_call_target="tpu_custom_call" | custom-call | flops 50331648000 | bytes 39321600 | tf_op jit(solution)/shard_map/stepped/pallas_call | solution.py:317
  197.0 29.6 %by_states.1.dy_ref = bf16[2048,640]{1,0:T(8,128)(2,1)} custom-call(bf16[2,2048,3200]{2,1,0:T(8,128)(2,1)} %get-tuple-element.14.t_ref, bf16[2048,640]{1,0:T(8,128)(2,1)} %forward.1.h_ref, bf16[2048,640]{1,0:T(8,128)(2,1)} %bitcast.31, bf16[2,640,3200]{2,1,0:T(8,128)(2,1)} %rest_0_.3, bf16[2,640,3200]{2,1,0:T(8,128)(2,1)} %rest_1_.3), custom_call_target="tpu_custom_call" | custom-call | flops 16777216000 | bytes 34406400 | tf_op jit(solution)/shard_map/by_states/pallas_call | solution.py:86
  226.6 152.8 %stepped.3 = (bf16[15,80,640]{2,1,0:T(8,128)(2,1)}, bf16[15,8,80,640]{3,2,1,0:T(8,128)(2,1)}) custom-call(bf16[2048,640]{1,0:T(8,128)(2,1)} %bitcast.33, bf16[2048,640]{1,0:T(8,128)(2,1)} %by_states.1.dy_ref, bf16[2,640,3200]{2,1,0:T(8,128)(2,1)} %rest_0_.3, bf16[2,640,3200]{2,1,0:T(8,128)(2,1)} %rest_1_.3, bf16[2,3200,640]{2,1,0:T(8,128)(2,1)} %rest_2_.3, ...), custom_call_target="tpu_custom_call" | custom-call | flops 50331648000 | bytes 39321600 | tf_op jit(solution)/shard_map/stepped/pallas_call | solution.py:317
  379.4 2.3 fusion.6
  381.7 0.1 copy.26
  381.9 0.0 copy-start.7
  381.9 0.6 stack_reshape.42
  382.5 0.2 copy.28
  382.7 1.4 stack_reshape.44
  384.1 0.0 copy-done.7
  384.1 1.1 fusion.7
  385.2 0.1 copy.27
  385.4 0.0 copy-start.2
  385.4 1.4 stack_reshape.43
  386.8 1.2 copy.29
  388.0 1.4 stack_reshape.45
  389.4 0.0 copy-done.2
  389.4 7.1 %fusion.3 = (f32[2,80,3200]{2,1,0:T(8,128)}, f32[2,80,3200]{2,1,0:T(8,128)}, f32[2,80,3200]{2,1,0:T(8,128)}, f32[2,80,3200]{2,1,0:T(8,128)}) fusion(f32[2,80,3200]{2,1,0:T(8,128)} %rest_6_.3, bf16[1,80,3200]{2,1,0:T(8,128)(2,1)} %stack_reshape.43, bf16[1,80,3200]{2,1,0:T(8,128)(2,1)S(1)} %stack_reshape.42, f32[2,80,3200]{2,1,0:T(8,128)S(1)} %copy-done.2, ...), kind=kLoop, calls=%fused_computation.18 | loop fusion | flops 9216000 | bytes 18432000 | tf_op jit(solution)/shard_map/add | solution.py:26
  396.5 7.5 %slice_bitcast_fusion.1 = (bf16[8,5,80,640]{3,2,0,1:T(8,128)(2,1)}, bf16[8,80,5,640]{3,1,0,2:T(8,128)(2,1)}, bf16[8,80,5,640]{3,1,0,2:T(8,128)(2,1)S(1)}) fusion(bf16[15,8,80,640]{3,2,1,0:T(8,128)(2,1)} %get-tuple-element.15), kind=kLoop, calls=%fused_computation.4 | loop fusion | bytes 24576000 | tf_op jit(solution)/shard_map/transpose | solution.py:369
  404.0 5.5 %copy.20 = bf16[8,80,5,640]{3,2,1,0:T(8,128)(2,1)} copy(bf16[8,80,5,640]{3,1,0,2:T(8,128)(2,1)S(1)} %get-tuple-element.21) | data formatting | bytes 8192000 | tf_op jit(solution)/shard_map/transpose | solution.py:366
  409.5 10.4 %stack_reshape.36 = bf16[1,640,3200]{2,1,0:T(8,128)(2,1)} reshape(bf16[8,80,5,640]{3,2,1,0:T(8,128)(2,1)} %copy.20) | data formatting | bytes 8192000 | tf_op jit(solution)/shard_map/stack;reshape | solution.py:374
  419.9 7.6 %copy.22 = bf16[8,80,5,640]{3,2,1,0:T(8,128)(2,1)} copy(bf16[8,80,5,640]{3,1,0,2:T(8,128)(2,1)} %get-tuple-element.20) | data formatting | bytes 8192000 | tf_op jit(solution)/shard_map/transpose | solution.py:366
  427.5 10.2 %stack_reshape.38 = bf16[1,640,3200]{2,1,0:T(8,128)(2,1)} reshape(bf16[8,80,5,640]{3,2,1,0:T(8,128)(2,1)} %copy.22) | data formatting | bytes 8192000 | tf_op jit(solution)/shard_map/stack;reshape | solution.py:374
  437.7 7.5 %slice_bitcast_fusion = (bf16[8,5,80,640]{3,2,0,1:T(8,128)(2,1)}, bf16[8,80,5,640]{3,1,0,2:T(8,128)(2,1)}, bf16[8,80,5,640]{3,1,0,2:T(8,128)(2,1)S(1)}) fusion(bf16[15,8,80,640]{3,2,1,0:T(8,128)(2,1)} %get-tuple-element.16), kind=kLoop, calls=%fused_computation.3 | loop fusion | bytes 24576000 | tf_op jit(solution)/shard_map/transpose | solution.py:369
  445.2 5.5 %copy.21 = bf16[8,80,5,640]{3,2,1,0:T(8,128)(2,1)} copy(bf16[8,80,5,640]{3,1,0,2:T(8,128)(2,1)S(1)} %get-tuple-element.24) | data formatting | bytes 8192000 | tf_op jit(solution)/shard_map/transpose | solution.py:366
  450.7 10.2 %stack_reshape.37 = bf16[1,640,3200]{2,1,0:T(8,128)(2,1)} reshape(bf16[8,80,5,640]{3,2,1,0:T(8,128)(2,1)} %copy.21) | data formatting | bytes 8192000 | tf_op jit(solution)/shard_map/stack;reshape | solution.py:374
  460.9 7.6 %copy.23 = bf16[8,80,5,640]{3,2,1,0:T(8,128)(2,1)} copy(bf16[8,80,5,640]{3,1,0,2:T(8,128)(2,1)} %get-tuple-element.23) | data formatting | bytes 8192000 | tf_op jit(solution)/shard_map/transpose | solution.py:366
  468.5 10.3 %stack_reshape.39 = bf16[1,640,3200]{2,1,0:T(8,128)(2,1)} reshape(bf16[8,80,5,640]{3,2,1,0:T(8,128)(2,1)} %copy.23) | data formatting | bytes 8192000 | tf_op jit(solution)/shard_map/stack;reshape | solution.py:374
  478.7 0.0 copy-start.3
  478.7 0.0 copy-start.4
  478.7 0.0 copy-start.5
  478.7 0.0 copy-start.6
  478.7 12.9 %pad_maximum_fusion = (bf16[2,640,3200]{2,1,0:T(8,128)(2,1)}, bf16[2,640,3200]{2,1,0:T(8,128)(2,1)}) fusion(bf16[1,640,3200]{2,1,0:T(8,128)(2,1)} %stack_reshape.37, bf16[1,640,3200]{2,1,0:T(8,128)(2,1)} %stack_reshape.36, bf16[1,640,3200]{2,1,0:T(8,128)(2,1)} %stack_reshape.39, bf16[1,640,3200]{2,1,0:T(8,128)(2,1)} %stack_reshape.38), kind=kLoop, calls=%fused_computation | loop fusion | flops 8192000 | bytes 32768000 | tf_op jit(solution)/shard_map/stack | solution.py:374
  491.6 0.0 copy-done.3
  491.6 0.0 copy-done.4
  491.6 0.0 copy-done.5
  491.6 0.0 copy-done.6
  491.6 0.0 copy-start
  491.7 2.7 fusion.5
  494.3 0.8 copy-done
  495.2 0.0 copy-start.1
  495.2 0.4 copy.24
  495.5 1.8 copy-done.1
  497.3 0.4 copy.25
  497.7 4.2 pad_maximum_fusion.2
Async XLA Ops:
  381.9 2.2 copy-start.7
  385.4 4.0 copy-start.2
  478.7 12.9 %copy-start.3 = (bf16[5,80,640]{2,1,0:T(8,128)(2,1)S(1)}, bf16[5,80,640]{2,1,0:T(8,128)(2,1)}, u32[]{:S(2)}) copy-start(bf16[5,80,640]{2,1,0:T(8,128)(2,1)} %get-tuple-element.25) | copy-start | bytes 1536004
  478.7 12.9 %copy-start.4 = (bf16[5,80,640]{2,1,0:T(8,128)(2,1)S(1)}, bf16[5,80,640]{2,1,0:T(8,128)(2,1)}, u32[]{:S(2)}) copy-start(bf16[5,80,640]{2,1,0:T(8,128)(2,1)} %get-tuple-element.28) | copy-start | bytes 1536004
  478.7 12.9 %copy-start.5 = (f32[2,400,640]{2,1,0:T(8,128)S(1)}, f32[2,400,640]{2,1,0:T(8,128)}, u32[]{:S(2)}) copy-start(f32[2,400,640]{2,1,0:T(8,128)} %rest_5_.3) | copy-start | bytes 6144004
  478.7 12.9 %copy-start.6 = (f32[2,400,640]{2,1,0:T(8,128)S(1)}, f32[2,400,640]{2,1,0:T(8,128)}, u32[]{:S(2)}) copy-start(f32[2,400,640]{2,1,0:T(8,128)} %rest_8_.3) | copy-start | bytes 6144004
  491.6 3.5 copy-start
  495.2 2.2 copy-start.1

commit v4 on v3

v4 whole, which is shorter than its diff:
```python
import functools

import jax
import jax.numpy as jnp
from jax import lax
from jax.experimental import pallas as pl
from jax.experimental.pallas import tpu as pltpu
from jax.sharding import PartitionSpec as P

NAMES = ("w_gate", "w_up", "w_down")
BF, F32 = jnp.bfloat16, jnp.float32
TILE = 512
LIMIT = 66_900_000


def dot(a, b, dims):
    return lax.dot_general(a, b, (dims, ((), ())), preferred_element_type=F32)


def normed(wide):
    return (wide * lax.rsqrt(jnp.mean(wide * wide, -1, keepdims=True) + 1e-6)).astype(BF)


def adamw(w, m, v, g):
    m = 0.9 * m + 0.1 * g
    v = 0.95 * v + 0.05 * g * g
    step = m * lax.rsqrt(v + 1e-8) + 0.1 * w
    return (w - 0.02 * step).astype(BF), m, v


def pieces(n, step):
    cuts = list(range(0, n - n % step, step)) + [n] if n % step else list(range(0, n + 1, step))
    if len(cuts) > 2 and cuts[-1] - cuts[-2] < step:
        del cuts[-2]
    return list(zip(cuts, cuts[1:]))


def whole(layer, rows, columns):
    return pl.BlockSpec((None, rows, columns), lambda t: (layer, 0, 0), pipeline_mode=pl.Buffered(1))


def tiles(columns):
    return pl.BlockSpec((TILE, columns), lambda t: (t, 0))


def forward(h, wg, wu, wd, layer):
    tokens, d = h.shape
    ff = wg.shape[-1]

    def kernel(h_ref, wg_ref, wu_ref, wd_ref, o_ref, mid_ref):
        wide = h_ref[...].astype(F32)
        a = normed(wide)
        total = jnp.zeros((TILE, d), F32)
        for lo, hi in pieces(ff, 768):
            gate = jnp.dot(a, wg_ref[:, lo:hi], preferred_element_type=F32)
            up = jnp.dot(a, wu_ref[:, lo:hi], preferred_element_type=F32)
            mid = (gate * jax.nn.sigmoid(gate) * up).astype(BF)
            mid_ref[:, lo:hi] = mid
            total += jnp.dot(mid, wd_ref[lo:hi, :], preferred_element_type=F32)
        o_ref[...] = (wide + total.astype(BF).astype(F32)).astype(BF)

    return pl.pallas_call(
        kernel,
        grid=(tokens // TILE,),
        in_specs=[tiles(d), whole(layer, d, ff), whole(layer, d, ff), whole(layer, ff, d)],
        out_specs=[tiles(d), tiles(ff)],
        out_shape=[jax.ShapeDtypeStruct((tokens, d), BF), jax.ShapeDtypeStruct((tokens, ff), BF)],
        compiler_params=pltpu.CompilerParams(vmem_limit_bytes=LIMIT),
        cost_estimate=pl.CostEstimate(flops=6 * tokens * d * ff, bytes_accessed=2 * 3 * d * ff, transcendentals=tokens * ff),
        name="forward",
    )(h, wg, wu, wd)


def stepped(x, h, mid0, dy, weights, ms, vs, size):
    tokens, d = h.shape
    layers, _, ff = weights[0].shape
    chips, rows = size // 2, d // size
    assert layers == 2 and chips == 4 and ff % d == 0 and ff // size % rows == 0 and d % size == 0
    cuts = ff // d
    blocks = 3 * cuts
    slots = 4 + cuts
    first = 48
    second = rows - first
    halves = (pl.ds(0, first), pl.ds(first, second))
    parts = 4
    tile = tokens // parts
    per = parts + 3
    lags = (1, 2, 4, 6, 8, 10, 12)
    made = per * cuts
    states_at = made
    down_at = states_at + parts * cuts
    again_at = down_at + cuts
    steps = again_at + made - 1 + lags[-1]
    MESH = pl.DeviceIdType.MESH

    def kernel(x_ref, h_ref, dy_ref, wg_ref, wu_ref, wd_ref, mid0_hbm, *rest):
        w_hbm, m_hbm, v_hbm = rest[:3], rest[3:6], rest[6:9]
        g_hbm, all_ref, two_hbm = rest[9:12]
        two, a_ref, a_t, dy_all, dy_t, mid, taken, by_g, by_u = rest[12:21]
        own, near, in_a, in_b, gnew, wnew, wold, mold, vold, send, recv, load, keep, away, fetch = rest[21:]
        t = pl.program_id(0)
        me = lax.axis_index("dp")
        chip, core = me // 2, me % 2
        partner = {"dp": me + 1 - 2 * core}

        def at(step):
            return lax.rem(chip + step + chips, chips)

        def dev(step):
            return at(step) * 2 + core

        def slot(q):
            return jnp.where(q < 2 * cuts, lax.rem(q, 4), q - 2 * cuts + 4)

        def copy(src, dst, kind, q, to):
            n = slot(q)
            return pltpu.make_async_remote_copy(
                src_ref=src, dst_ref=dst, send_sem=send.at[kind, n], recv_sem=recv.at[kind, n], device_id=to, device_id_type=MESH
            )

        def way(q):
            return 1 - 2 * lax.rem(q, 2)

        def over(q):
            return copy(own.at[slot(q), :, 1 - core], near.at[slot(q)], 0, q, partner)

        def message(q, kind, second):
            step = -way(q) if second == (kind != 1) else way(q)
            c = at(2) if kind == 0 else at(step)
            into = in_b if second else in_a
            return copy(own.at[slot(q), c, core, halves[second], :], into.at[slot(q), kind], 1 + 2 * kind + second, q, {"dp": dev(step)})

        def part(q, c, half):
            return own[slot(q), c, core, half, :].astype(F32) + near[slot(q), c, half, :].astype(F32)

        def there(n, q, step):
            return copy(wnew.at[slot(q)], all_ref.at[n, q, me], 7 if step == 1 else 8, q, {"dp": dev(step)})

        def onward(n, q, second):
            step = -way(q) if second else way(q)
            where = all_ref.at[n, q, dev(-step), halves[second], :]
            return copy(where, where, 9 + second, q, {"dp": dev(step)})

        def across(n, q, step):
            where = all_ref.at[n, q, dev(step)]
            return copy(where if step else wnew.at[slot(q)], where, 11 + step + (step < 0) * 4, q, partner)

        def kept(n, q):
            return (
                pltpu.make_async_copy(wnew.at[slot(q)], all_ref.at[n, q, me], keep.at[slot(q), 0]),
                pltpu.make_async_copy(gnew.at[slot(q)], g_hbm.at[n, q], keep.at[slot(q), 1]),
            )

        def loads(n, q, which):
            k = slot(q)
            if which < 2:
                columns = pl.ds(pl.multiple_of(q // 2 * d, 128), d)
                mine, ours = (pl.ds(0, rows), columns), (pl.ds(pl.multiple_of(me * rows, 16), rows), columns)
            else:
                b = jnp.maximum(q - 2 * cuts, 0)
                mine = pl.ds(pl.multiple_of(b * rows, 16), rows), pl.ds(0, d)
                ours = pl.ds(pl.multiple_of(me * (ff // size) + b * rows, 16), rows), pl.ds(0, d)
            return (
                pltpu.make_async_copy(w_hbm[which].at[(n, *ours)], wold.at[k], load.at[k, 0]),
                pltpu.make_async_copy(m_hbm[which].at[(n, *mine)], mold.at[k], load.at[k, 1]),
                pltpu.make_async_copy(v_hbm[which].at[(n, *mine)], vold.at[k], load.at[k, 2]),
            )

        @pl.when(t == 0)
        def _():
            barrier = pltpu.get_barrier_semaphore()
            for to in (partner, {"dp": dev(1)}, {"dp": dev(-1)}):
                pl.semaphore_signal(barrier, inc=1, device_id=to, device_id_type=MESH)
            pl.semaphore_wait(barrier, 3)

        def begin(n, q):
            over(q).start()
            for which, on in enumerate(
                (
                    jnp.logical_and(q < 2 * cuts, lax.rem(q, 2) == 0),
                    jnp.logical_and(q < 2 * cuts, lax.rem(q, 2) == 1),
                    q >= 2 * cuts,
                )
            ):

                @pl.when(on)
                def _(which=which):
                    for one in loads(n, q, which):
                        one.start()

        def split(n, q):
            over(q).wait()
            for kind in (0, 1):
                for second in (0, 1):
                    step = -way(q) if second == (kind != 1) else way(q)
                    c = at(2) if kind == 0 else at(step)
                    own[slot(q), c, core, halves[second], :] = part(q, c, halves[second]).astype(BF)
            for kind in (0, 1):
                for second in (0, 1):
                    message(q, kind, second).start()

        def join(n, q):
            for second, into in ((0, in_a), (1, in_b)):
                message(q, 0, second).wait_recv()
                c = at(-way(q) if second else way(q))
                total = part(q, c, halves[second]) + into[slot(q), 0].astype(F32)
                own[slot(q), c, core, halves[second], :] = total.astype(BF)
            for second in (0, 1):
                message(q, 2, second).start()

        def update(n, q):
            for kind in (1, 2):
                for second in (0, 1):
                    message(q, kind, second).wait_recv()
            for one in loads(n, q, 2):
                one.wait()
            k = slot(q)
            for second, into in ((0, in_a), (1, in_b)):
                half = halves[second]
                g = (part(q, chip, half) + into[k, 1].astype(F32) + into[k, 2].astype(F32)).astype(BF)
                gnew[k, half, :] = g
                wnew[k, half, :] = adamw(wold[k, half, :].astype(F32), mold[k, half, :], vold[k, half, :], g.astype(F32))[0]
            there(n, q, 1).start()
            there(n, q, -1).start()
            across(n, q, 0).start()
            for one in kept(n, q):
                one.start()

        def relay(n, q):
            there(n, q, 1).wait_recv()
            there(n, q, -1).wait_recv()
            onward(n, q, 0).start()
            onward(n, q, 1).start()
            across(n, q, 1).start()
            across(n, q, -1).start()

        def rest_of(n, q):
            onward(n, q, 0).wait_recv()
            onward(n, q, 1).wait_recv()
            across(n, q, 2).start()

        def close(n, q):
            for step in (0, 1, -1, 2):
                across(n, q, step).wait()
            for one in kept(n, q):
                one.wait()
            for kind in range(3):
                for second in (0, 1):
                    message(q, kind, second).wait_send()
            there(n, q, 1).wait_send()
            there(n, q, -1).wait_send()
            onward(n, q, 0).wait_send()
            onward(n, q, 1).wait_send()

        def inside(e, lo, hi):
            return jnp.logical_and(e >= lo, e < hi)

        for lag, act in reversed(tuple(zip(lags, (begin, split, join, update, relay, rest_of, close)))):
            e = t - lag
            n = jnp.where(e < again_at - 1, 1, 0)
            late = e - jnp.where(n == 1, made - 1, again_at - 1)
            pl.when(inside(late, 0, cuts))(functools.partial(act, n, 2 * cuts + late))
            n = jnp.where(e < again_at, 1, 0)
            e = e - jnp.where(n == 1, 0, again_at)
            r = lax.rem(e, per)
            pl.when(jnp.logical_and(inside(e, 0, made), inside(r, parts, parts + 2)))(functools.partial(act, n, 2 * (e // per) + r - parts))

        last = t < states_at
        i = t - jnp.where(last, 0, again_at)
        b, r = i // per, lax.rem(i, per)
        on = inside(i, 0, made)

        def out_copy(b):
            return pltpu.make_async_copy(two, two_hbm.at[:, :, pl.ds(pl.multiple_of(b * d, 128), d)], away)

        def fetched(i):
            where = two_hbm.at[:, pl.ds(pl.multiple_of(i // cuts * tile, tile), tile), pl.ds(pl.multiple_of(lax.rem(i, cuts) * d, 128), d)]
            return pltpu.make_async_copy(where, taken.at[lax.rem(i, 2)], fetch.at[lax.rem(i, 2)])

        def product(i):
            where = mid0_hbm.at[:, pl.ds(pl.multiple_of(i * d, 128), d)]
            return pltpu.make_async_copy(where, two.at[lax.rem(i, 2)], fetch.at[lax.rem(i, 2)])

        def spread(g, b):
            for p in range(size):
                n = b * size + p
                owner = n // cuts
                own[4 + lax.rem(n, cuts), owner // 2, lax.rem(owner, 2)] = g[p * rows : (p + 1) * rows]

        @pl.when(jnp.logical_and(last, jnp.logical_and(r == 0, b > 0)))
        def _():
            out_copy(b - 1).wait()

        @pl.when(jnp.logical_and(on, r < parts))
        def _():
            here = pl.ds(pl.multiple_of(r * tile, tile), tile)

            @pl.when(b == 0)
            def _():
                @pl.when(last)
                def _():
                    a_ref[here, :] = normed(h_ref[...].astype(F32))
                    dy_all[here, :] = dy_ref[...]
                    dy_t[:, here] = dy_ref[...].T

                @pl.when(jnp.logical_not(last))
                def _():
                    a_ref[here, :] = normed(x_ref[...].astype(F32))

                a_t[:, here] = a_ref[here, :].T

            a = a_ref[here, :]
            gate = jnp.dot(a, wg_ref[...], preferred_element_type=F32)
            up = jnp.dot(a, wu_ref[...], preferred_element_type=F32)
            s = jax.nn.sigmoid(gate)
            silu = gate * s
            mid[here, :] = (silu * up).astype(BF)
            dmid = dot(dy_all[here, :], wd_ref[...], ((1,), (1,))).astype(BF).astype(F32)
            two[0, here, :] = (dmid * up * (s * (1 + gate * (1 - s)))).astype(BF)
            two[1, here, :] = (dmid * silu).astype(BF)

            @pl.when(jnp.logical_and(last, r == parts - 1))
            def _():
                out_copy(b).start()

        @pl.when(jnp.logical_and(on, inside(r, parts, parts + 2)))
        def _():
            g = jnp.dot(a_t[...], two[r - parts], preferred_element_type=F32).astype(BF)
            own[slot(2 * b + r - parts)] = g.reshape(chips, 2, rows, d)

        @pl.when(jnp.logical_and(last, r == per - 1))
        def _():
            spread(jnp.dot(dy_t[...], mid[...], preferred_element_type=F32).astype(BF).T, b)

        @pl.when(t == states_at - 1)
        def _():
            out_copy(cuts - 1).wait()
            fetched(0).start()

        j = t - states_at

        @pl.when(inside(j, 0, parts * cuts))
        def _():
            k = lax.rem(j, cuts)
            fetched(j).wait()

            @pl.when(j < parts * cuts - 1)
            def _():
                fetched(j + 1).start()

            @pl.when(j == parts * cuts - 1)
            def _():
                product(0).start()

            at_g = dot(taken[lax.rem(j, 2), 0], wg_ref[...], ((1,), (1,)))
            at_u = dot(taken[lax.rem(j, 2), 1], wu_ref[...], ((1,), (1,)))

            @pl.when(k == 0)
            def _():
                by_g[...] = at_g
                by_u[...] = at_u

            @pl.when(k > 0)
            def _():
                by_g[...] += at_g
                by_u[...] += at_u

            @pl.when(k == cuts - 1)
            def _():
                here = pl.ds(pl.multiple_of(j // cuts * tile, tile), tile)
                da = (by_g[...].astype(BF).astype(F32) + by_u[...].astype(BF).astype(F32)).astype(BF).astype(F32)
                wide = h_ref[...].astype(F32)
                scale = lax.rsqrt(jnp.mean(wide * wide, -1, keepdims=True) + 1e-6)
                inner = jnp.mean(da * wide, -1, keepdims=True)
                back = (da * scale - wide * (inner * scale * scale * scale)).astype(BF)
                new = (dy_all[here, :].astype(F32) + back.astype(F32)).astype(BF)
                dy_all[here, :] = new
                dy_t[:, here] = new.T

        @pl.when(inside(t, down_at, again_at))
        def _():
            k = t - down_at
            product(k).wait()

            @pl.when(k < cuts - 1)
            def _():
                product(k + 1).start()

            spread(jnp.dot(dy_t[...], two[lax.rem(k, 2)], preferred_element_type=F32).astype(BF).T, k)

    def block(t):
        again = jnp.clip(jnp.maximum(t - again_at, 0) // per, 0, cuts - 1)
        b = jnp.where(t < states_at, t // per, jnp.where(t < down_at, lax.rem(jnp.maximum(t - states_at, 0), cuts), again))
        return jnp.where(t < down_at, 1, 0), b

    def at_states(t):
        return jnp.where(t < states_at, jnp.minimum(t, parts - 1), jnp.minimum((t - states_at) // cuts, parts - 1)), 0

    wide = pl.BlockSpec((None, d, d), lambda t: (block(t)[0], 0, block(t)[1]))
    tall = pl.BlockSpec((None, d, d), lambda t: (*block(t), 0))
    hbm = pl.BlockSpec(memory_space=pl.ANY)
    return pl.pallas_call(
        kernel,
        grid=(steps,),
        in_specs=[
            pl.BlockSpec((tile, d), lambda t: (jnp.clip(t - again_at, 0, parts - 1), 0)),
            pl.BlockSpec((tile, d), at_states),
            pl.BlockSpec((tile, d), lambda t: (jnp.minimum(t, parts - 1), 0)),
            wide,
            wide,
            tall,
        ]
        + [hbm] * 10,
        out_specs=[hbm] * 3,
        out_shape=[
            jax.ShapeDtypeStruct((layers, blocks, rows, d), BF),
            jax.ShapeDtypeStruct((layers, blocks, size, rows, d), BF),
            jax.ShapeDtypeStruct((2, tokens, ff), BF),
        ],
        scratch_shapes=[
            pltpu.VMEM((2, tokens, d), BF),
            pltpu.VMEM((tokens, d), BF),
            pltpu.VMEM((d, tokens), BF),
            pltpu.VMEM((tokens, d), BF),
            pltpu.VMEM((d, tokens), BF),
            pltpu.VMEM((tokens, d), BF),
            pltpu.VMEM((2, 2, tile, d), BF),
            pltpu.VMEM((tile, d), F32),
            pltpu.VMEM((tile, d), F32),
            pltpu.VMEM((slots, chips, 2, rows, d), BF),
            pltpu.VMEM((slots, chips, rows, d), BF),
            pltpu.VMEM((slots, 3, first, d), BF),
            pltpu.VMEM((slots, 3, second, d), BF),
            pltpu.VMEM((slots, rows, d), BF),
            pltpu.VMEM((slots, rows, d), BF),
            pltpu.VMEM((slots, rows, d), BF),
            pltpu.VMEM((slots, rows, d), F32),
            pltpu.VMEM((slots, rows, d), F32),
            pltpu.SemaphoreType.DMA((15, slots)),
            pltpu.SemaphoreType.DMA((15, slots)),
            pltpu.SemaphoreType.DMA((slots, 3)),
            pltpu.SemaphoreType.DMA((slots, 2)),
            pltpu.SemaphoreType.DMA,
            pltpu.SemaphoreType.DMA((2,)),
        ],
        compiler_params=pltpu.CompilerParams(vmem_limit_bytes=LIMIT, collective_id=0, has_side_effects=True),
        cost_estimate=pl.CostEstimate(flops=26 * tokens * d * ff, bytes_accessed=4 * 3 * tokens * ff, transcendentals=0),
        name="stepped",
    )(x, h, dy, *weights, mid0, *weights, *ms, *vs)


def assembled(gathered):
    layers, blocks, size, rows, d = gathered.shape
    cuts = blocks // 3
    ff = cuts * d

    def kernel(ref, g_ref, u_ref, d_ref):
        for p in range(2):
            for b in range(cuts):
                g_ref[p * rows : (p + 1) * rows, b * d : (b + 1) * d] = ref[2 * b, p]
                u_ref[p * rows : (p + 1) * rows, b * d : (b + 1) * d] = ref[2 * b + 1, p]
                d_ref[(p * cuts + b) * rows : (p * cuts + b + 1) * rows, :] = ref[2 * cuts + b, p]

    wide = pl.BlockSpec((None, 2 * rows, ff), lambda n, p: (n, p, 0))
    tall = pl.BlockSpec((None, 2 * ff // size, d), lambda n, p: (n, p, 0))
    return pl.pallas_call(
        kernel,
        grid=(layers, size // 2),
        in_specs=[pl.BlockSpec((None, blocks, 2, rows, d), lambda n, p: (n, 0, p, 0, 0))],
        out_specs=[wide, wide, tall],
        out_shape=[jax.ShapeDtypeStruct((layers, d, ff), BF)] * 2 + [jax.ShapeDtypeStruct((layers, ff, d), BF)],
        name="assembled",
    )(gathered)


def moments(sums, ms, vs):
    layers, blocks, rows, d = sums.shape
    cuts = blocks // 3

    def kernel(g_ref, *refs):
        b = pl.program_id(1)
        for i, q in enumerate((2 * b, 2 * b + 1, 2 * cuts + b)):
            g = g_ref[q].astype(F32)
            _, refs[6 + i][...], refs[9 + i][...] = adamw(jnp.zeros_like(g), refs[i][...], refs[3 + i][...], g)

    wide = pl.BlockSpec((None, rows, d), lambda n, b: (n, 0, b))
    tall = pl.BlockSpec((None, rows, d), lambda n, b: (n, b, 0))
    return pl.pallas_call(
        kernel,
        grid=(layers, cuts),
        in_specs=[pl.BlockSpec((None, blocks, rows, d), lambda n, b: (n, 0, 0, 0))] + [wide, wide, tall] * 2,
        out_specs=[wide, wide, tall] * 2,
        out_shape=[jax.ShapeDtypeStruct(t.shape, F32) for t in ms] * 2,
        name="moments",
    )(sums, *ms, *vs)


def solution(mesh):
    size = mesh.shape["dp"]

    def body(x, dy, *arrays):
        weights, ms, vs = (arrays[i : i + 3] for i in (0, 3, 6))
        h, mid0 = forward(x[0], *weights, 0)
        sums, gathered, _ = stepped(x[0], h, mid0, dy[0], weights, ms, vs, size)
        return (*assembled(gathered), *moments(sums, ms, vs))

    rows = P(None, "dp", None)
    seqs = P(("rep", "dp"), None, None)
    return jax.shard_map(
        body,
        mesh=mesh,
        in_specs=(seqs, seqs, P(), P(), P()) + (rows,) * 6,
        out_specs=(P("rep", None, None),) * 3 + (P("rep", "dp", None),) * 6,
        check_vma=False,
    )
```

time: 509 us -> 384 us (0.75); the launches traced: 502 us -> 384 us
  local copies, waits for them, and re-layouts: 95.5 us -> 0 us
  other arithmetic: 26.9 us -> 0 us
    another operation x8 -> x0, local copies, waits for them, and re-layouts: 45.9 us -> none  [the longest x4 41 us: body(): out = [jnp.stack(one) for one in zip(*map(each, gathered))]]
    transpose x12 -> x0, local copies, waits for them, and re-layouts: 43.5 us -> none  [the longest x8 27.7 us: wide(): return jnp.moveaxis(t, 0, -2).reshape(-1, ff)]
    another operation x2 -> x0, other arithmetic: 17.1 us -> none  [body(): out = [jnp.stack(one) for one in zip(*map(each, gathered))]]
    add x2 -> x0, other arithmetic: 9.83 us -> none  [adamw(): v = 0.95 * v + 0.05 * g * g]
where the time goes in v4:
time: 384 us
  Pallas kernels  383 us (100%)
    pallas_call x1, Pallas kernels, stepped(): pl.pallas_call(kernel, grid=(steps,), in_specs=[pl.BlockSpec((tile, d), l...  314 us
    pallas_call x1, Pallas kernels, forward(): pl.pallas_call(kernel, grid=(tokens // TILE,), in_specs=[tiles(d), whole(...  38.8 us
    pallas_call x1, Pallas kernels, assembled(): pl.pallas_call(kernel, grid=(layers, size // 2), in_specs=[pl.BlockSpec((...  18.1 us
    pallas_call x1, Pallas kernels, moments(): pl.pallas_call(kernel, grid=(layers, cuts), in_specs=[pl.BlockSpec((None,...  12.4 us

profile of v4, /device:TPU:113, one launch (start us, length us, event | category | flops | bytes accessed | tf_op | source)
XLA Modules:
  0.0 384.0 jit_solution(11236666187165853254)
XLA Ops:
  0.6 38.8 %forward.1 = (bf16[2048,640]{1,0:T(8,128)(2,1)}, bf16[2048,3200]{1,0:T(8,128)(2,1)}) custom-call(bf16[2048,640]{1,0:T(8,128)(2,1)} %bitcast.2, bf16[2,640,3200]{2,1,0:T(8,128)(2,1)} %rest_0_.1, bf16[2,640,3200]{2,1,0:T(8,128)(2,1)} %rest_1_.1, bf16[2,3200,640]{2,1,0:T(8,128)(2,1)} %rest_2_.1), custom_call_target="tpu_custom_call" | custom-call | flops 25165824000 | bytes 12288000 | tf_op jit(solution)/shard_map/forward/pallas_call | solution.py:62
  39.5 313.8 %stepped.1 = (bf16[2,15,80,640]{3,2,1,0:T(8,128)(2,1)}, bf16[2,15,8,80,640]{4,3,2,1,0:T(8,128)(2,1)}, bf16[2,2048,3200]{2,1,0:T(8,128)(2,1)}) custom-call(bf16[2048,640]{1,0:T(8,128)(2,1)} %bitcast.3, bf16[2048,640]{1,0:T(8,128)(2,1)} %get-tuple-element.22.h_ref, bf16[2048,640]{1,0:T(8,128)(2,1)} %bitcast.4, bf16[2,640,3200]{2,1,0:T(8,128)(2,1)} %rest_0_.1, ...), custom_call_target="tpu_custom_call" | custom-call | flops 109051904000 | bytes 78643200 | tf_op jit(solution)/shard_map/stepped/pallas_call | solution.py:402
  353.3 18.1 %assembled.1 = (bf16[2,640,3200]{2,1,0:T(8,128)(2,1)}, bf16[2,640,3200]{2,1,0:T(8,128)(2,1)}, bf16[2,3200,640]{2,1,0:T(8,128)(2,1)}) custom-call(bf16[2,15,8,80,640]{4,3,2,1,0:T(8,128)(2,1)} %get-tuple-element.24.ref), custom_call_target="tpu_custom_call" | custom-call | tf_op jit(solution)/shard_map/assembled/pallas_call | solution.py:466
  371.5 12.4 %moments.1 = (f32[2,80,3200]{2,1,0:T(8,128)}, f32[2,80,3200]{2,1,0:T(8,128)}, f32[2,400,640]{2,1,0:T(8,128)}, f32[2,80,3200]{2,1,0:T(8,128)}, f32[2,80,3200]{2,1,0:T(8,128)}, /*index=5*/f32[2,400,640]{2,1,0:T(8,128)}) custom-call(bf16[2,15,80,640]{3,2,1,0:T(8,128)(2,1)} %get-tuple-element.28.g_ref, f32[2,80,3200]{2,1,0:T(8,128)} %refs_0_.1, ...), custom_call_target="tpu_custom_call" | custom-call | tf_op jit(solution)/shard_map/moments/pallas_call | solution.py:488

commit v5 on v4

--- a/solution.py
+++ b/solution.py
@@ -78,26 +78,31 @@
     assert layers == 2 and chips == 4 and ff % d == 0 and ff // size % rows == 0 and d % size == 0
     cuts = ff // d
     blocks = 3 * cuts
-    slots = 4 + cuts
+    early = 6
+    slots = early + cuts
     first = 48
     second = rows - first
     halves = (pl.ds(0, first), pl.ds(first, second))
-    parts = 4
+    parts = 2
     tile = tokens // parts
-    per = parts + 3
-    lags = (1, 2, 4, 6, 8, 10, 12)
+    small = tile // 2
+    per = parts + 2
+    lags = (1, 2, 4, 7, 9, 11, 12)
+    space = 1
+    held = 2
     made = per * cuts
     states_at = made
-    down_at = states_at + parts * cuts
-    again_at = down_at + cuts
-    steps = again_at + made - 1 + lags[-1]
+    again_at = states_at + parts * cuts
+    down_at = again_at + held * per
+    steps = again_at + cuts + made - 1 + lags[-1]
+    assert down_at >= made - 1 + space * (cuts - 1) + lags[-1] and 2 * early >= 2 * cuts and early // 2 * per >= lags[-1]
     MESH = pl.DeviceIdType.MESH
 
     def kernel(x_ref, h_ref, dy_ref, wg_ref, wu_ref, wd_ref, mid0_hbm, *rest):
         w_hbm, m_hbm, v_hbm = rest[:3], rest[3:6], rest[6:9]
         g_hbm, all_ref, two_hbm = rest[9:12]
-        two, a_ref, a_t, dy_all, dy_t, mid, taken, by_g, by_u = rest[12:21]
-        own, near, in_a, in_b, gnew, wnew, wold, mold, vold, send, recv, load, keep, away, fetch = rest[21:]
+        two, a_ref, a_t, dy_all, dy_t, mid, by_g, by_u = rest[12:20]
+        own, near, in_a, in_b, gnew, wnew, wold, mold, vold, send, recv, load, keep, away, fetch = rest[20:]
         t = pl.program_id(0)
         me = lax.axis_index("dp")
         chip, core = me // 2, me % 2
@@ -110,7 +115,7 @@
             return at(step) * 2 + core
 
         def slot(q):
-            return jnp.where(q < 2 * cuts, lax.rem(q, 4), q - 2 * cuts + 4)
+            return jnp.where(q < early, q, jnp.where(q < 2 * cuts, q - early, q - 2 * cuts + early))
 
         def copy(src, dst, kind, q, to):
             n = slot(q)
@@ -255,37 +260,57 @@
         def inside(e, lo, hi):
             return jnp.logical_and(e >= lo, e < hi)
 
+        def again(e):
+            return jnp.where(e < down_at, e - again_at, jnp.where(e < down_at + cuts, -1, e - again_at - cuts))
+
         for lag, act in reversed(tuple(zip(lags, (begin, split, join, update, relay, rest_of, close)))):
             e = t - lag
-            n = jnp.where(e < again_at - 1, 1, 0)
-            late = e - jnp.where(n == 1, made - 1, again_at - 1)
-            pl.when(inside(late, 0, cuts))(functools.partial(act, n, 2 * cuts + late))
+            n = jnp.where(e < down_at + cuts - 1, 1, 0)
+            late = e - jnp.where(n == 1, made - 1, down_at + cuts - 1)
+            on = jnp.logical_and(inside(late, 0, cuts * space), lax.rem(late, space) == 0)
+            pl.when(on)(functools.partial(act, n, 2 * cuts + late // space))
             n = jnp.where(e < again_at, 1, 0)
-            e = e - jnp.where(n == 1, 0, again_at)
-            r = lax.rem(e, per)
-            pl.when(jnp.logical_and(inside(e, 0, made), inside(r, parts, parts + 2)))(functools.partial(act, n, 2 * (e // per) + r - parts))
+            e = jnp.where(n == 1, e, again(e))
+
+            @pl.when(jnp.logical_and(inside(e, 0, made), lax.rem(e, per) == parts))
+            def _(act=act, n=n, e=e):
+                b = e // per
+                act(n, 2 * b)
+                act(n, 2 * b + 1)
 
         last = t < states_at
-        i = t - jnp.where(last, 0, again_at)
+        i = jnp.where(last, t, again(t))
         b, r = i // per, lax.rem(i, per)
         on = inside(i, 0, made)
 
         def out_copy(b):
             return pltpu.make_async_copy(two, two_hbm.at[:, :, pl.ds(pl.multiple_of(b * d, 128), d)], away)
 
+        def turn(i):
+            j = jnp.where(i < cuts, 0, 1)
+            return j, i - j * cuts
+
         def fetched(i):
-            where = two_hbm.at[:, pl.ds(pl.multiple_of(i // cuts * tile, tile), tile), pl.ds(pl.multiple_of(lax.rem(i, cuts) * d, 128), d)]
-            return pltpu.make_async_copy(where, taken.at[lax.rem(i, 2)], fetch.at[lax.rem(i, 2)])
+            j, k = turn(i)
+            n = lax.rem(i, 2)
+            return [
+                pltpu.make_async_copy(
+                    two_hbm.at[which, pl.ds(pl.multiple_of(j * tile, tile), tile), pl.ds(pl.multiple_of(k * d, 128), d)],
+                    two.at[n, pl.ds(which * tile, tile)],
+                    fetch.at[n, which],
+                )
+                for which in range(2)
+            ]
 
         def product(i):
             where = mid0_hbm.at[:, pl.ds(pl.multiple_of(i * d, 128), d)]
-            return pltpu.make_async_copy(where, two.at[lax.rem(i, 2)], fetch.at[lax.rem(i, 2)])
+            return pltpu.make_async_copy(where, two.at[lax.rem(i, 2)], fetch.at[lax.rem(i, 2), 0])
 
         def spread(g, b):
             for p in range(size):
                 n = b * size + p
                 owner = n // cuts
-                own[4 + lax.rem(n, cuts), owner // 2, lax.rem(owner, 2)] = g[p * rows : (p + 1) * rows]
+                own[early + lax.rem(n, cuts), owner // 2, lax.rem(owner, 2)] = g[p * rows : (p + 1) * rows]
 
         @pl.when(jnp.logical_and(last, jnp.logical_and(r == 0, b > 0)))
         def _():
@@ -293,40 +318,49 @@
 
         @pl.when(jnp.logical_and(on, r < parts))
         def _():
-            here = pl.ds(pl.multiple_of(r * tile, tile), tile)
-
-            @pl.when(b == 0)
-            def _():
-                @pl.when(last)
+            def one(piece, _):
+                here = pl.ds(pl.multiple_of(r * tile + piece * small, small), small)
+                there = pl.ds(pl.multiple_of(piece * small, small), small)
+
+                @pl.when(b == 0)
                 def _():
-                    a_ref[here, :] = normed(h_ref[...].astype(F32))
-                    dy_all[here, :] = dy_ref[...]
-                    dy_t[:, here] = dy_ref[...].T
-
-                @pl.when(jnp.logical_not(last))
-                def _():
-                    a_ref[here, :] = normed(x_ref[...].astype(F32))
-
-                a_t[:, here] = a_ref[here, :].T
-
-            a = a_ref[here, :]
-            gate = jnp.dot(a, wg_ref[...], preferred_element_type=F32)
-            up = jnp.dot(a, wu_ref[...], preferred_element_type=F32)
-            s = jax.nn.sigmoid(gate)
-            silu = gate * s
-            mid[here, :] = (silu * up).astype(BF)
-            dmid = dot(dy_all[here, :], wd_ref[...], ((1,), (1,))).astype(BF).astype(F32)
-            two[0, here, :] = (dmid * up * (s * (1 + gate * (1 - s)))).astype(BF)
-            two[1, here, :] = (dmid * silu).astype(BF)
+                    @pl.when(last)
+                    def _():
+                        a_ref[here, :] = normed(h_ref[there, :].astype(F32))
+                        dy_all[here, :] = dy_ref[there, :]
+                        dy_t[:, here] = dy_ref[there, :].T
+
+                    @pl.when(jnp.logical_not(last))
+                    def _():
+                        a_ref[here, :] = normed(x_ref[there, :].astype(F32))
+
+                    a_t[:, here] = a_ref[here, :].T
+
+                a = a_ref[here, :]
+                gate = jnp.dot(a, wg_ref[...], preferred_element_type=F32)
+                up = jnp.dot(a, wu_ref[...], preferred_element_type=F32)
+                s = jax.nn.sigmoid(gate)
+                silu = gate * s
+                mid[here, :] = (silu * up).astype(BF)
+                dmid = dot(dy_all[here, :], wd_ref[...], ((1,), (1,))).astype(BF).astype(F32)
+                two[0, here, :] = (dmid * up * (s * (1 + gate * (1 - s)))).astype(BF)
+                two[1, here, :] = (dmid * silu).astype(BF)
+                return 0
+
+            lax.fori_loop(0, 2, one, 0)
 
             @pl.when(jnp.logical_and(last, r == parts - 1))
             def _():
                 out_copy(b).start()
 
-        @pl.when(jnp.logical_and(on, inside(r, parts, parts + 2)))
-        def _():
-            g = jnp.dot(a_t[...], two[r - parts], preferred_element_type=F32).astype(BF)
-            own[slot(2 * b + r - parts)] = g.reshape(chips, 2, rows, d)
+        @pl.when(jnp.logical_and(on, r == parts))
+        def _():
+            def one(which, _):
+                g = jnp.dot(a_t[...], two[which], preferred_element_type=F32).astype(BF)
+                own[slot(2 * b + which)] = g.reshape(chips, 2, rows, d)
+                return 0
+
+            lax.fori_loop(0, 2, one, 0)
 
         @pl.when(jnp.logical_and(last, r == per - 1))
         def _():
@@ -335,49 +369,51 @@
         @pl.when(t == states_at - 1)
         def _():
             out_copy(cuts - 1).wait()
-            fetched(0).start()
+            for one in fetched(0):
+                one.start()
 
         j = t - states_at
 
         @pl.when(inside(j, 0, parts * cuts))
         def _():
-            k = lax.rem(j, cuts)
-            fetched(j).wait()
+            which, k = turn(j)
+            for one in fetched(j):
+                one.wait()
 
             @pl.when(j < parts * cuts - 1)
             def _():
-                fetched(j + 1).start()
-
-            @pl.when(j == parts * cuts - 1)
-            def _():
-                product(0).start()
-
-            at_g = dot(taken[lax.rem(j, 2), 0], wg_ref[...], ((1,), (1,)))
-            at_u = dot(taken[lax.rem(j, 2), 1], wu_ref[...], ((1,), (1,)))
+                for one in fetched(j + 1):
+                    one.start()
 
             @pl.when(k == 0)
             def _():
-                by_g[...] = at_g
-                by_u[...] = at_u
-
-            @pl.when(k > 0)
-            def _():
-                by_g[...] += at_g
-                by_u[...] += at_u
+                by_g[...] = jnp.zeros_like(by_g)
+                by_u[...] = jnp.zeros_like(by_u)
+
+            for piece in range(2):
+                there = pl.ds(piece * small, small)
+                by_g[there, :] += dot(two[lax.rem(j, 2), there, :], wg_ref[...], ((1,), (1,)))
+                by_u[there, :] += dot(two[lax.rem(j, 2), pl.ds(tile + piece * small, small), :], wu_ref[...], ((1,), (1,)))
 
             @pl.when(k == cuts - 1)
             def _():
-                here = pl.ds(pl.multiple_of(j // cuts * tile, tile), tile)
-                da = (by_g[...].astype(BF).astype(F32) + by_u[...].astype(BF).astype(F32)).astype(BF).astype(F32)
-                wide = h_ref[...].astype(F32)
-                scale = lax.rsqrt(jnp.mean(wide * wide, -1, keepdims=True) + 1e-6)
-                inner = jnp.mean(da * wide, -1, keepdims=True)
-                back = (da * scale - wide * (inner * scale * scale * scale)).astype(BF)
-                new = (dy_all[here, :].astype(F32) + back.astype(F32)).astype(BF)
-                dy_all[here, :] = new
-                dy_t[:, here] = new.T
-
-        @pl.when(inside(t, down_at, again_at))
+                for piece in range(2):
+                    here = pl.ds(pl.multiple_of(which * tile + piece * small, small), small)
+                    there = pl.ds(piece * small, small)
+                    da = (by_g[there, :].astype(BF).astype(F32) + by_u[there, :].astype(BF).astype(F32)).astype(BF).astype(F32)
+                    wide = h_ref[there, :].astype(F32)
+                    scale = lax.rsqrt(jnp.mean(wide * wide, -1, keepdims=True) + 1e-6)
+                    inner = jnp.mean(da * wide, -1, keepdims=True)
+                    back = (da * scale - wide * (inner * scale * scale * scale)).astype(BF)
+                    new = (dy_all[here, :].astype(F32) + back.astype(F32)).astype(BF)
+                    dy_all[here, :] = new
+                    dy_t[:, here] = new.T
+
+        @pl.when(t == down_at - 1)
+        def _():
+            product(0).start()
+
+        @pl.when(inside(t, down_at, down_at + cuts))
         def _():
             k = t - down_at
             product(k).wait()
@@ -389,12 +425,13 @@
             spread(jnp.dot(dy_t[...], two[lax.rem(k, 2)], preferred_element_type=F32).astype(BF).T, k)
 
     def block(t):
-        again = jnp.clip(jnp.maximum(t - again_at, 0) // per, 0, cuts - 1)
-        b = jnp.where(t < states_at, t // per, jnp.where(t < down_at, lax.rem(jnp.maximum(t - states_at, 0), cuts), again))
-        return jnp.where(t < down_at, 1, 0), b
+        again = jnp.where(t < down_at, t - again_at, jnp.maximum(t - again_at - cuts, held * per - 1))
+        again = jnp.clip(jnp.maximum(again, 0) // per, 0, cuts - 1)
+        b = jnp.where(t < states_at, t // per, jnp.where(t < again_at, lax.rem(jnp.maximum(t - states_at, 0), cuts), again))
+        return jnp.where(t < again_at, 1, 0), b
 
     def at_states(t):
-        return jnp.where(t < states_at, jnp.minimum(t, parts - 1), jnp.minimum((t - states_at) // cuts, parts - 1)), 0
+        return jnp.where(t < states_at, jnp.minimum(t, parts - 1), jnp.where(t < states_at + cuts, 0, 1)), 0
 
     wide = pl.BlockSpec((None, d, d), lambda t: (block(t)[0], 0, block(t)[1]))
     tall = pl.BlockSpec((None, d, d), lambda t: (*block(t), 0))
@@ -403,9 +440,9 @@
         kernel,
         grid=(steps,),
         in_specs=[
-            pl.BlockSpec((tile, d), lambda t: (jnp.clip(t - again_at, 0, parts - 1), 0)),
-            pl.BlockSpec((tile, d), at_states),
-            pl.BlockSpec((tile, d), lambda t: (jnp.minimum(t, parts - 1), 0)),
+            pl.BlockSpec((tile, d), lambda t: (jnp.clip(t - again_at, 0, parts - 1), 0), pipeline_mode=pl.Buffered(1)),
+            pl.BlockSpec((tile, d), at_states, pipeline_mode=pl.Buffered(1)),
+            pl.BlockSpec((tile, d), lambda t: (jnp.minimum(t, parts - 1), 0), pipeline_mode=pl.Buffered(1)),
             wide,
             wide,
             tall,
@@ -424,7 +461,6 @@
             pltpu.VMEM((tokens, d), BF),
             pltpu.VMEM((d, tokens), BF),
             pltpu.VMEM((tokens, d), BF),
-            pltpu.VMEM((2, 2, tile, d), BF),
             pltpu.VMEM((tile, d), F32),
             pltpu.VMEM((tile, d), F32),
             pltpu.VMEM((slots, chips, 2, rows, d), BF),
@@ -441,7 +477,7 @@
             pltpu.SemaphoreType.DMA((slots, 3)),
             pltpu.SemaphoreType.DMA((slots, 2)),
             pltpu.SemaphoreType.DMA,
-            pltpu.SemaphoreType.DMA((2,)),
+            pltpu.SemaphoreType.DMA((2, 2)),
         ],
         compiler_params=pltpu.CompilerParams(vmem_limit_bytes=LIMIT, collective_id=0, has_side_effects=True),
         cost_estimate=pl.CostEstimate(flops=26 * tokens * d * ff, bytes_accessed=4 * 3 * tokens * ff, transcendentals=0),

time: 384 us -> 364 us (0.948)
  Pallas kernels: 383 us -> 363 us
    pallas_call x1, Pallas kernels: 314 us -> 293 us  [stepped(): pl.pallas_call(kernel, grid=(steps,), in_specs=[pl.BlockSpec((tile, d), l...]
where the time goes in v5:
time: 364 us; the launch traced here: 363 us
  Pallas kernels  363 us (100%)
    pallas_call x1, Pallas kernels, stepped(): pl.pallas_call(kernel, grid=(steps,), in_specs=[pl.BlockSpec((tile, d), l...  293 us
    pallas_call x1, Pallas kernels, forward(): pl.pallas_call(kernel, grid=(tokens // TILE,), in_specs=[tiles(d), whole(...  38.8 us
    pallas_call x1, Pallas kernels, assembled(): pl.pallas_call(kernel, grid=(layers, size // 2), in_specs=[pl.BlockSpec((...  18.1 us
    pallas_call x1, Pallas kernels, moments(): pl.pallas_call(kernel, grid=(layers, cuts), in_specs=[pl.BlockSpec((None,...  12.4 us

profile of v5, /device:TPU:113, one launch (start us, length us, event | category | flops | bytes accessed | tf_op | source)
XLA Modules:
  0.0 363.4 jit_solution(223306014943997224)
XLA Ops:
  0.6 38.8 %forward.1 = (bf16[2048,640]{1,0:T(8,128)(2,1)}, bf16[2048,3200]{1,0:T(8,128)(2,1)}) custom-call(bf16[2048,640]{1,0:T(8,128)(2,1)} %bitcast.2, bf16[2,640,3200]{2,1,0:T(8,128)(2,1)} %rest_0_.1, bf16[2,640,3200]{2,1,0:T(8,128)(2,1)} %rest_1_.1, bf16[2,3200,640]{2,1,0:T(8,128)(2,1)} %rest_2_.1), custom_call_target="tpu_custom_call" | custom-call | flops 25165824000 | bytes 12288000 | tf_op jit(solution)/shard_map/forward/pallas_call | solution.py:62
  39.5 293.2 %stepped.1 = (bf16[2,15,80,640]{3,2,1,0:T(8,128)(2,1)}, bf16[2,15,8,80,640]{4,3,2,1,0:T(8,128)(2,1)}, bf16[2,2048,3200]{2,1,0:T(8,128)(2,1)}) custom-call(bf16[2048,640]{1,0:T(8,128)(2,1)} %bitcast.3, bf16[2048,640]{1,0:T(8,128)(2,1)} %get-tuple-element.22.h_ref, bf16[2048,640]{1,0:T(8,128)(2,1)} %bitcast.4, bf16[2,640,3200]{2,1,0:T(8,128)(2,1)} %rest_0_.1, ...), custom_call_target="tpu_custom_call" | custom-call | flops 109051904000 | bytes 78643200 | tf_op jit(solution)/shard_map/stepped/pallas_call | solution.py:439
  332.7 18.1 %assembled.1 = (bf16[2,640,3200]{2,1,0:T(8,128)(2,1)}, bf16[2,640,3200]{2,1,0:T(8,128)(2,1)}, bf16[2,3200,640]{2,1,0:T(8,128)(2,1)}) custom-call(bf16[2,15,8,80,640]{4,3,2,1,0:T(8,128)(2,1)} %get-tuple-element.24.ref), custom_call_target="tpu_custom_call" | custom-call | tf_op jit(solution)/shard_map/assembled/pallas_call | solution.py:502
  350.9 12.4 %moments.1 = (f32[2,80,3200]{2,1,0:T(8,128)}, f32[2,80,3200]{2,1,0:T(8,128)}, f32[2,400,640]{2,1,0:T(8,128)}, f32[2,80,3200]{2,1,0:T(8,128)}, f32[2,80,3200]{2,1,0:T(8,128)}, /*index=5*/f32[2,400,640]{2,1,0:T(8,128)}) custom-call(bf16[2,15,80,640]{3,2,1,0:T(8,128)(2,1)} %get-tuple-element.28.g_ref, f32[2,80,3200]{2,1,0:T(8,128)} %refs_0_.1, ...), custom_call_target="tpu_custom_call" | custom-call | tf_op jit(solution)/shard_map/moments/pallas_call | solution.py:524
